TPU v7x, 256 devices: a 2x2x32 block of a 4x8x32 slice. The times are simulated.
256 devices in a mesh: parts: 4 (over y, x), ka: 64 (over z, core).
Axes of the slice: x: 2, y: 2, z: 32, core: 2. Of those that a mesh axis runs over, the one named last changes fastest.
The devices are a block of a 4x8x32 slice.
Arguments:
- energies: float32 [256, 200], P(('parts', 'ka')), parts along dimension 0, may hold values from -4 to 4
- proj: float32 [256, 2, 10, 200], P(('parts', 'ka')), parts along dimension 0, may hold values from -0.3125 to 0.3125
- window: int32 [256, 2], P(('parts', 'ka')), parts along dimension 0, may hold values from 0 to 200, as said below
- sigma: float32 [8, 10, 10, 256], P('parts', None, None, 'ka'), parts along dimension 0, may hold values from -3 to 1.5, as said below
- impurity_inverse: float32 [8, 10, 10, 256], P('parts', None, None, 'ka'), parts along dimension 0, may hold values from -5 to 50, as said below
Outputs:
- density: float32 [256, 2, 200, 200], P(('parts', 'ka')), parts along dimension 0
- sigma_new: float32 [8, 10, 10, 256], P('parts', None, None, 'ka'), parts along dimension 0
There are 4 independent parts, one for each index of `parts`. A program takes and returns all parts, laid end to end along the dimension named above; each array names one. Nothing has to cross between parts.
Inputs may be any that keep to these rules, and one draw needn't show every extreme that they name: window[k, 0] < 40 and window[k, 1] >= 160 for every k-point. For every frequency, sigma[0] and sigma[1] are real symmetric matrices and -sigma[1] is positive definite with smallest eigenvalue 0.2 or more. For every frequency n, impurity_inverse[0] and impurity_inverse[1] are real symmetric matrices and impurity_inverse[1] + sigma[1] - freqs[n] times the identity is positive definite with smallest eigenvalue 0.2 or more.
All inputs are finite; a program needn't handle non-finite values.
Results may differ from a plain program's by a relative error of at most 0.00011.
Values sent between devices are 32-bit elements; how exact they have to be, the bound alone decides.
No kernel may reach another device: no remote copies, remote signals or barrier semaphores. Data moves between devices by JAX's collectives and lax.ppermute only.
A program may use at most 64 MiB of HBM per device.

v0:
```python
import math

import jax
import jax.numpy as jnp
from jax import lax
from jax.experimental import pallas as pl
from jax.experimental.pallas import tpu as pltpu
from jax.sharding import Mesh
from jax.sharding import PartitionSpec as P

highest = lax.Precision.HIGHEST
inverse_temp = 40.0
LANES = 128
NN = (((1,), (0,)), ((), ()))
NT = (((1,), (1,)), ((), ()))


def tail_weight(count):
    total = 0.0
    for number in range(count):
        total += (inverse_temp / (math.pi * (2 * number + 1))) ** 2
    return inverse_temp / 4.0 - 2.0 / inverse_temp * total


def dot(a, b, dims, precision=highest):
    return lax.dot_general(a, b, dims, precision=precision, preferred_element_type=jnp.float32)


def split(x):
    high = x.astype(jnp.bfloat16)
    return high, (x - high.astype(jnp.float32)).astype(jnp.bfloat16)


def dot3(a, b, dims):
    return sum(
        lax.dot_general(x, y, dims, preferred_element_type=jnp.float32)
        for x, y in ((a[0], b[0]), (a[0], b[1]), (a[1], b[0]))
    )


def iota(shape, dim):
    return lax.broadcasted_iota(jnp.int32, shape, dim)


def matsubara(number):
    return (2.0 * number.astype(jnp.float32) + 1.0) * (math.pi / inverse_temp)


def masked_projector(proj_ref, window_ref):
    proj_re = proj_ref[0, 0]
    proj_im = proj_ref[0, 1]
    band = iota(proj_re.shape, 1)
    inside = (band >= window_ref[0, 0]) & (band < window_ref[0, 1])
    return jnp.where(inside, proj_re, 0.0), jnp.where(inside, proj_im, 0.0)


def invert(mat_re, mat_im):
    size = len(mat_re)
    mat_re, mat_im = list(mat_re), list(mat_im)
    column = iota(mat_re[0].shape, 0)
    for p in range(size):
        at = column == p
        piv_re = mat_re[p][p : p + 1]
        piv_im = mat_im[p][p : p + 1]
        rec = 1.0 / (piv_re * piv_re + piv_im * piv_im)
        rec_re = piv_re * rec
        rec_im = -piv_im * rec
        old_re = jnp.where(at, 1.0, mat_re[p])
        old_im = jnp.where(at, 0.0, mat_im[p])
        row_re = old_re * rec_re - old_im * rec_im
        row_im = old_re * rec_im + old_im * rec_re
        for i in range(size):
            if i == p:
                continue
            col_re = mat_re[i][p : p + 1]
            col_im = mat_im[i][p : p + 1]
            rest_re = jnp.where(at, 0.0, mat_re[i])
            rest_im = jnp.where(at, 0.0, mat_im[i])
            mat_re[i] = rest_re - (col_re * row_re - col_im * row_im)
            mat_im[i] = rest_im - (col_re * row_im + col_im * row_re)
        mat_re[p] = row_re
        mat_im[p] = row_im
    return mat_re, mat_im


def cmul(first_re, first_im, second_re, second_im):
    size = len(first_re)
    out_re, out_im = [], []
    for i in range(size):
        sum_re = sum_im = 0.0
        for k in range(size):
            a_re = first_re[i][k : k + 1]
            a_im = first_im[i][k : k + 1]
            sum_re = sum_re + (a_re * second_re[k] - a_im * second_im[k])
            sum_im = sum_im + (a_re * second_im[k] + a_im * second_re[k])
        out_re.append(sum_re)
        out_im.append(sum_im)
    return out_re, out_im


def rows_of(block, norb):
    return [block[norb * i : norb * (i + 1)] for i in range(norb)]


def turned(ref, first, chips, freqs, pitch):
    rows = [ref[pl.ds(first + f, chips, stride=pitch), :] for f in range(freqs)]
    return jnp.concatenate(rows, axis=0).T


def project_kernel(norb, chips, freqs, core_axis, energy_ref, proj_ref, window_ref, out_ref):
    core = lax.axis_index(core_axis)
    proj_re, proj_im = masked_projector(proj_ref, window_ref)
    pair = iota((LANES, norb), 0)
    orb = iota((LANES, norb), 1)
    first = sum((pair >= norb * t).astype(jnp.int32) for t in range(1, norb))
    inside = pair < norb * norb
    pick_i = jnp.where((first == orb) & inside, 1.0, 0.0)
    pick_j = jnp.where((pair - norb * first == orb) & inside, 1.0, 0.0)
    i_re, i_im = dot(pick_i, proj_re, NN), dot(pick_i, proj_im, NN)
    j_re, j_im = dot(pick_j, proj_re, NN), dot(pick_j, proj_im, NN)
    pair_re = i_re * j_re + i_im * j_im
    pair_im = i_im * j_re - i_re * j_im
    energy = energy_ref[...]
    group = 2 * freqs
    rows = chips * group
    for other in range(2):
        row = iota((rows, energy.shape[1]), 0)
        chip = row // group
        place = row - group * chip
        half = place // freqs
        number = 2 * freqs * chip + freqs * (core ^ other) + place - freqs * half
        freq = matsubara(number)
        denom = energy * energy + freq * freq
        green_re = -energy / denom
        green_im = -freq / denom
        real = half == 0
        total = dot(jnp.where(real, green_re, green_im), pair_re, NT) + dot(
            jnp.where(real, -green_im, green_re), pair_im, NT
        )
        out_ref[:, group * other : group * (other + 1), :] = total.reshape(chips, group, LANES)


def dyson_kernel(
    norb, chips, freqs, points, own_ref, sib_ref, sigma_ref, imp_ref, new_ref, tile_ref,
    mat_ref, sum_ref, small_ref, wide_ref, turn_ref,
):
    pairs = norb * norb
    group = 2 * freqs
    for half in range(2):
        mat_ref[half, :, :LANES] = turned(own_ref, freqs * half, chips, freqs, 2 * group)
        mat_ref[half, :, LANES:] = turned(sib_ref, freqs * half, chips, freqs, group)
    for which, ref in enumerate((sigma_ref, imp_ref)):
        for half in range(2):
            for i in range(norb):
                at = (which * 2 + half) * pairs + norb * i
                small_ref[at : at + norb, :] = ref[half, i]
    spread = jnp.where(iota((freqs, LANES), 1) // chips == iota((freqs, LANES), 0), 1.0, 0.0)
    wide_ref[...] = dot(small_ref[...], spread, NN)

    def rows(ref, base):
        return [ref[base + norb * i : base + norb * (i + 1), :] for i in range(norb)]

    sig_re, sig_im = rows(wide_ref, 0), rows(wide_ref, pairs)
    for part in range(2):
        lanes = pl.ds(LANES * part, LANES)
        mat = [
            [mat_ref[half, norb * i : norb * (i + 1), lanes] for i in range(norb)]
            for half in range(2)
        ]
        ainv_re, ainv_im = invert(*mat)
        gorb_re, gorb_im = invert(
            [a - s for a, s in zip(ainv_re, sig_re)], [a - s for a, s in zip(ainv_im, sig_im)]
        )
        for i in range(norb):
            sum_ref[norb * i : norb * (i + 1), lanes] = gorb_re[i]
            sum_ref[pairs + norb * i : pairs + norb * (i + 1), lanes] = gorb_im[i]
    both = sum_ref[:, :LANES] + sum_ref[:, LANES:]
    same = iota((LANES, LANES), 0) // chips == iota((LANES, LANES), 1) // chips
    sum_ref[:, :LANES] = dot(both, jnp.where(same, 1.0 / points, 0.0), NN)
    loc = [
        [sum_ref[base + norb * i : base + norb * (i + 1), :LANES] for i in range(norb)]
        for base in (0, pairs)
    ]
    inv = invert(*loc)
    imp = rows(wide_ref, 2 * pairs), rows(wide_ref, 3 * pairs)
    pitch = turn_ref.shape[1] // norb
    diff = [[v - m for v, m in zip(inv[half], imp[half])] for half in range(2)]
    for half in range(2):
        for i in range(norb):
            turn_ref[half, pitch * i : pitch * i + norb, :] = diff[half][i]
    mat_ref[...] = jnp.zeros_like(mat_ref)
    for half, sig, sign in ((0, sig_re, 1.0), (1, sig_im, -1.0)):
        for i in range(norb):
            across = turn_ref[half, pl.ds(i, norb, stride=pitch), :]
            fresh = sig[i] + 0.5 * (diff[half][i] + sign * across)
            mat_ref[half, norb * i : norb * (i + 1), :LANES] = fresh
    lane = iota((LANES, freqs), 0)
    pick = jnp.where(lane == chips * iota((LANES, freqs), 1), 1.0, 0.0)
    for half in range(2):
        few = dot(mat_ref[half, :, :LANES], pick, NN)
        for i in range(norb):
            new_ref[half, i] = few[norb * i : norb * (i + 1)]
    row = iota((group, LANES), 0)
    lane = iota((group, LANES), 1)
    tile = 0.0
    for half in range(2):
        choose = jnp.where(lane == chips * (row - freqs * half), 1.0, 0.0)
        tile = tile + dot(choose, mat_ref[half, :, :LANES], NT)
    tile_ref[...] = jnp.broadcast_to(tile[None], tile_ref.shape)


def density_kernel(
    norb, chips, freqs, core_axis, energy_ref, proj_ref, window_ref, mat_ref, own_ref, sib_ref,
    out_ref, flat_ref, ainv_ref, sig_ref, vert_ref, sums_ref,
):
    core = lax.axis_index(core_axis)
    group = 2 * freqs
    bands = energy_ref.shape[1]
    count = 2 * freqs * chips
    tall = -(-bands // 16) * 16
    pad = flat_ref.shape[1] // 8
    proj_re, proj_im = masked_projector(proj_ref, window_ref)
    flat_ref[...] = jnp.zeros_like(flat_ref)
    step = 16
    flat_ref[0:norb, :bands] = proj_re
    flat_ref[step : step + norb, :bands] = proj_im
    flat_ref[2 * step : 2 * step + 1, :bands] = energy_ref[...]
    upright = flat_ref[...].T[:tall]
    flat_ref[...] = jnp.zeros_like(flat_ref)
    flat_ref[0:norb, :bands] = -proj_im
    flat_ref[step : step + norb, :bands] = proj_re
    crossed = flat_ref[...].T[:tall]
    energy = upright[:, 2 * step : 2 * step + 1]
    lane = iota((tall, count), 1)
    part = lane // LANES
    within = lane - LANES * part
    place = within // chips
    number = 2 * freqs * (within - chips * place) + freqs * (core ^ part) + place
    freq = matsubara(number)
    denom = energy * energy + freq * freq
    green_re = -energy / denom
    green_im = -freq / denom
    last = number[:norb] == count - 1

    for part in range(2):
        lanes = pl.ds(LANES * part, LANES)
        for half in range(2):
            ainv_ref[half] = turned(mat_ref, group * part + freqs * half, chips, freqs, 2 * group)
            sig_ref[half, :, lanes] = turned(
                (own_ref, sib_ref)[part], freqs * half, chips, freqs, group
            )
        mat = [
            [ainv_ref[half, norb * i : norb * (i + 1), :] for i in range(norb)] for half in range(2)
        ]
        sig = [
            [sig_ref[half, norb * i : norb * (i + 1), lanes] for i in range(norb)]
            for half in range(2)
        ]
        inv = invert(*mat)
        dressed = invert(
            [a - s for a, s in zip(inv[0], sig[0])], [a - s for a, s in zip(inv[1], sig[1])]
        )
        whole = cmul(*cmul(*sig, *dressed), *sig)
        for i in range(norb):
            spot = pl.ds(count * i + LANES * part, LANES)
            vert_ref[0:norb, spot] = sig[0][i] + whole[0][i]
            vert_ref[step : step + norb, spot] = sig[1][i] + whole[1][i]

    spare = jnp.zeros((step - norb, norb * count), jnp.float32)
    vert_ref[norb:step] = spare
    vert_ref[step + norb : 2 * step] = spare
    orb = iota((norb, LANES), 1)
    ends = []
    for half in range(2):
        end = jnp.zeros((norb, LANES), jnp.float32)
        for i in range(norb):
            entry = jnp.where(last, sig_ref[half, norb * i : norb * (i + 1), :], 0.0)
            end = jnp.where(orb == i, jnp.sum(entry, axis=1, keepdims=True), end)
        ends.append(end)
        ends.append(jnp.zeros((step - norb, LANES), jnp.float32))
    end = jnp.concatenate(ends, axis=0)

    wide = 2 * step
    plus = upright[:, :wide]
    cross = crossed[:, :wide]
    to_re = jnp.where(iota(plus.shape, 1) < step, plus, -plus)
    to_im = jnp.where(iota(plus.shape, 1) < step, -cross, cross)
    left = jnp.concatenate([to_re, to_im], axis=0)
    left_parts = split(left)
    left_all = jnp.concatenate([left_parts[0], left_parts[0], left_parts[1]], axis=1)

    weight = -0.5 * inverse_temp * tail_weight(count)
    tail = weight * dot(left, end, NN)
    tail_re, tail_im = tail[:tall], tail[tall:]
    slot = iota((tall, LANES), 1) < norb
    side_re = jnp.where(slot, upright, 0.0)
    side_im = jnp.where(slot, crossed, 0.0)
    side_re, side_im, tail_re, tail_im = (split(x) for x in (side_re, side_im, tail_re, tail_im))

    total_re = dot3(side_re, tail_re, NT) - dot3(side_im, tail_im, NT)
    total_im = dot3(side_re, tail_im, NT) + dot3(side_im, tail_re, NT)
    for i in range(norb):
        vert = split(vert_ref[:, count * i : count * (i + 1)])
        vert_all = jnp.concatenate([vert[0], vert[1], vert[0]], axis=0)
        mixed = lax.dot_general(left_all, vert_all, NN, preferred_element_type=jnp.float32)
        mix_re, mix_im = mixed[:tall], mixed[tall:]
        right_re = mix_re * green_re - mix_im * green_im
        right_im = mix_re * green_im + mix_im * green_re
        p_re = upright[:, i : i + 1]
        p_im = -crossed[:, i : i + 1]
        side_re = green_re * p_re + green_im * p_im
        side_im = green_im * p_re - green_re * p_im
        side = split(jnp.concatenate([side_re, side_im], axis=1))
        total_re = total_re + dot3(side, split(jnp.concatenate([right_re, -right_im], axis=1)), NT)
        total_im = total_im + dot3(side, split(jnp.concatenate([right_im, right_re], axis=1)), NT)
    sums_ref[...] = jnp.zeros_like(sums_ref)
    for half, total, sign in ((0, total_re, 1.0), (1, total_im, -1.0)):
        sums_ref[:tall, :tall] = total
        both = sums_ref[...] + sign * sums_ref[...].T
        out_ref[0, half] = both[:bands, :bands] / inverse_temp


VMEM = pl.BlockSpec(memory_space=pltpu.VMEM)
SMEM = pl.BlockSpec(memory_space=pltpu.SMEM)


def f32(*shape):
    return jax.ShapeDtypeStruct(shape, jnp.float32)


def scratch(*shape):
    return pltpu.VMEM(shape, jnp.float32)


def local(energies, proj, window, sigma, impurity_inverse):
    norb = proj.shape[2]
    bands = energies.shape[1]
    freqs = sigma.shape[3]
    chips = lax.axis_size("z")
    cores = lax.axis_size("core")
    group = 2 * freqs
    pairs = norb * norb
    count = freqs * chips * cores
    points = energies.shape[0] * chips * cores
    swap = [(0, 1), (1, 0)]
    wide = -(-bands // LANES) * LANES
    roomy = pltpu.CompilerParams(vmem_limit_bytes=48 * 1024 * 1024)

    def run(body, out, specs, scratches=()):
        return pl.pallas_call(
            body,
            out_shape=out,
            in_specs=specs,
            out_specs=jax.tree.map(lambda _: VMEM, out),
            scratch_shapes=scratches,
            compiler_params=roomy,
        )

    def project(*refs):
        project_kernel(norb, chips, freqs, "core", *refs)

    def dyson(*refs):
        dyson_kernel(norb, chips, freqs, points, *refs)

    def rebuild(*refs):
        density_kernel(norb, chips, freqs, "core", *refs)

    mats = run(project, f32(chips, 2 * group, LANES), [VMEM, VMEM, SMEM])(energies, proj, window)
    got = lax.all_to_all(mats, "z", 0, 0, tiled=True)
    sib = lax.ppermute(got[:, group:], "core", swap)
    sigma_new, tiles = run(
        dyson,
        (f32(2, norb, norb, freqs), f32(chips, group, LANES)),
        [VMEM] * 4,
        [
            scratch(2, LANES, 2 * LANES),
            scratch(2 * pairs, 2 * LANES),
            scratch(4 * pairs, freqs),
            scratch(4 * pairs, LANES),
            scratch(2, 16 * norb, LANES),
        ],
    )(got.reshape(-1, LANES), sib.reshape(-1, LANES), sigma, impurity_inverse)
    own = lax.all_to_all(tiles, "z", 0, 0, tiled=True)
    sib = lax.ppermute(own, "core", swap)
    density = run(
        rebuild,
        f32(1, 2, bands, bands),
        [VMEM, VMEM, SMEM, VMEM, VMEM, VMEM],
        [
            scratch(LANES, wide),
            scratch(2, LANES, LANES),
            scratch(2, LANES, 2 * LANES),
            scratch(32, norb * count),
            scratch(wide, wide),
        ],
    )(
        energies,
        proj,
        window,
        mats.reshape(-1, LANES),
        own.reshape(-1, LANES),
        sib.reshape(-1, LANES),
    )
    return density, sigma_new


def solution(mesh):
    parts, line = mesh.shape["parts"], mesh.shape["ka"]
    torus = Mesh(mesh.devices.reshape(parts, line // 2, 2), ("parts", "z", "core"))
    every = ("parts", "z", "core")
    line = ("z", "core")
    in_specs = (
        P(every, None),
        P(every, None, None, None),
        P(every, None),
        P("parts", None, None, line),
        P("parts", None, None, line),
    )
    out_specs = (P(every, None, None, None), P("parts", None, None, line))
    return jax.shard_map(local, mesh=torus, in_specs=in_specs, out_specs=out_specs, check_vma=False)
```

profile of v0, /device:TPU:37, one launch (start us, length us, event | category | flops | bytes accessed | tf_op | source)
XLA Modules:
  0.0 130.2 jit_solution(8803970774637458262)
XLA Ops:
  0.6 0.0 copy-start.1
  0.6 0.0 copy-start
  0.6 0.7 copy.10.refs_1_
  1.4 0.0 copy-done.1
  1.4 0.0 copy-done
  1.4 2.4 %shard_map.68 = f32[32,16,128]{2,1,0:T(8,128)S(1)} custom-call(f32[1,200]{1,0:T(1,128)S(1)} %copy-done, f32[1,2,10,200]{3,2,1,0:T(8,128)S(1)} %copy.10.refs_1_, s32[1,2]{1,0:T(1,128)S(1)} %copy-done.1), custom_call_target="tpu_custom_call" | custom-call | tf_op jit(solution)/shard_map/pallas_call | solution.py:368
  3.8 74.0 %all_to_all.10 = f32[32,16,128]{2,1,0:T(8,128)S(1)} all-to-all(f32[32,16,128]{2,1,0:T(8,128)S(1)} %shard_map.68), channel_id=1, replica_groups=mesh['parts'=4,'z'=32,'core'=2] {'z'}, dimensions={0} | all-to-all | bytes 524288 | tf_op jit(solution)/shard_map/all_to_all | solution.py:369
  77.7 0.0 copy-start.2
  77.8 0.0 copy-start.3
  77.8 2.0 %collective-permute-start = (f32[32,8,128]{2,1,0:T(8,128)S(1)}, f32[32,8,128]{2,1,0:T(8,128)S(1)}, u32[]{:S(2)}, u32[]{:S(2)}) collective-permute-start(f32[32,8,128]{2,1,0:T(8,128)S(1)} %slice.4), channel_id=1, source_target_pairs={{0,1},{1,0},{2,3},{3,2},{4,5},{5,4},{6,7},{7,6},{8,9},{9,8},{10,11... | collective-permute-start | bytes 393224 | tf_op jit(solution)/shard_map/ppermute | solution.py:370
  79.7 0.0 copy-done.2
  79.7 0.2 copy.8.refs_2_
  80.0 0.0 copy-done.3
  80.0 0.2 copy.9.refs_3_
  80.2 0.5 collective-permute-done
  80.7 2.7 %shard_map.69 = (f32[2,10,10,4]{3,2,1,0:T(8,128)S(1)}, f32[32,8,128]{2,1,0:T(8,128)S(1)}) custom-call(f32[512,128]{1,0:T(8,128)S(1)} %bitcast.6, f32[256,128]{1,0:T(8,128)S(1)} %bitcast.8, f32[2,10,10,4]{3,2,1,0:T(8,128)S(1)} %copy.8.refs_2_, f32[2,10,10,4]{3,2,1,0:T(8,128)S(1)} %copy.9.refs_3_), custom_call_target="tpu_custom_call" | custom-call | tf_op jit(solution)/shard_map/pallas_call | solution.py:371
  83.5 33.2 %all_to_all.11 = f32[32,8,128]{2,1,0:T(8,128)S(1)} all-to-all(f32[32,8,128]{2,1,0:T(8,128)S(1)} %get-tuple-element.4), channel_id=1, replica_groups=mesh['parts'=4,'z'=32,'core'=2] {'z'}, dimensions={0} | all-to-all | bytes 262144 | tf_op jit(solution)/shard_map/all_to_all | solution.py:383
  116.7 2.5 %collective-permute-start.1 = (f32[32,8,128]{2,1,0:T(8,128)S(1)}, f32[32,8,128]{2,1,0:T(8,128)S(1)}, u32[]{:S(2)}, u32[]{:S(2)}) collective-permute-start(f32[32,8,128]{2,1,0:T(8,128)S(1)} %all_to_all.11), channel_id=1, source_target_pairs={{0,1},{1,0},{2,3},{3,2},{4,5},{5,4},{6,7},{7,6},{8,9},{9,8},{10,11... | collective-permute-start | bytes 393224 | tf_op jit(solution)/shard_map/ppermute | solution.py:384
  119.1 0.8 copy.11
  119.9 0.1 collective-permute-done.1
  120.1 10.1 %shard_map.70 = f32[1,2,200,200]{3,2,1,0:T(8,128)} custom-call(f32[1,200]{1,0:T(1,128)S(1)} %copy-done, f32[1,2,10,200]{3,2,1,0:T(8,128)S(1)} %copy.10.refs_1_, s32[1,2]{1,0:T(1,128)S(1)} %copy-done.1, f32[512,128]{1,0:T(8,128)S(1)} %bitcast.5, f32[256,128]{1,0:T(8,128)S(1)} %bitcast.7, f32[256,128]{1,0:T(8,128)S(1)} %bitcast.9), custom_call_target="tpu_custom_call" | custom-call | tf_op jit(solution)/shard_map/pallas_call | solution.py:385
  (1 shorter events, 0.0 us)
Async XLA Ops:
  0.6 0.8 copy-start.1
  0.6 0.8 copy-start
  77.7 2.0 %copy-start.2 = (f32[2,10,10,4]{2,3,1,0:T(4,128)S(1)}, f32[2,10,10,4]{2,3,1,0:T(4,128)}, u32[]{:S(2)}) copy-start(f32[2,10,10,4]{2,3,1,0:T(4,128)} %param.8) | copy-start | bytes 9604
  77.8 2.2 %copy-start.3 = (f32[2,10,10,4]{2,3,1,0:T(4,128)S(1)}, f32[2,10,10,4]{2,3,1,0:T(4,128)}, u32[]{:S(2)}) copy-start(f32[2,10,10,4]{2,3,1,0:T(4,128)} %param.9) | copy-start | bytes 9604
  77.8 3.0 %collective-permute-start = (f32[32,8,128]{2,1,0:T(8,128)S(1)}, f32[32,8,128]{2,1,0:T(8,128)S(1)}, u32[]{:S(2)}, u32[]{:S(2)}) collective-permute-start(f32[32,8,128]{2,1,0:T(8,128)S(1)} %slice.4), channel_id=1, source_target_pairs={{0,1},{1,0},{2,3},{3,2},{4,5},{5,4},{6,7},{7,6},{8,9},{9,8},{10,11... | collective-permute-start | bytes 393224 | tf_op jit(solution)/shard_map/ppermute | solution.py:370
  116.7 3.4 %collective-permute-start.1 = (f32[32,8,128]{2,1,0:T(8,128)S(1)}, f32[32,8,128]{2,1,0:T(8,128)S(1)}, u32[]{:S(2)}, u32[]{:S(2)}) collective-permute-start(f32[32,8,128]{2,1,0:T(8,128)S(1)} %all_to_all.11), channel_id=1, source_target_pairs={{0,1},{1,0},{2,3},{3,2},{4,5},{5,4},{6,7},{7,6},{8,9},{9,8},{10,11... | collective-permute-start | bytes 393224 | tf_op jit(solution)/shard_map/ppermute | solution.py:384
where the time goes:
time: 130 us
  blocking collectives  107 us (82%)
  Pallas kernels  15.2 us (12%)
  starting transfers between devices  4.42 us (3%)
  local copies, waits for them, and re-layouts  2.08 us (2%)
    all_to_all x1, blocking collectives, local(): got = lax.all_to_all(mats, 'z', 0, 0, tiled=True)  74 us
    all_to_all x1, blocking collectives, local(): own = lax.all_to_all(tiles, 'z', 0, 0, tiled=True)  33.2 us
    pallas_call x1, Pallas kernels, local(): run(rebuild, f32(1, 2, bands, bands), [VMEM, VMEM, SMEM, VMEM, VMEM, VMEM...  10.1 us
    pallas_call x1, Pallas kernels, local(): run(dyson, (f32(2, norb, norb, freqs), f32(chips, group, LANES)), [VMEM]...  2.75 us
  transfers between devices with their start and end apart: 2, of which 2 were waited for; matrix products, arithmetic and copies ran while one was open for 1% of the time, Pallas kernels for 0%

commit v1 on v0

v1 whole, which is shorter than its diff:
```python
import math

import jax
import jax.numpy as jnp
from jax import lax
from jax.experimental import pallas as pl
from jax.experimental.pallas import tpu as pltpu
from jax.sharding import Mesh
from jax.sharding import PartitionSpec as P

highest = lax.Precision.HIGHEST
inverse_temp = 40.0
LANES = 128
NN = (((1,), (0,)), ((), ()))
NT = (((1,), (1,)), ((), ()))


def tail_weight(count):
    total = 0.0
    for number in range(count):
        total += (inverse_temp / (math.pi * (2 * number + 1))) ** 2
    return inverse_temp / 4.0 - 2.0 / inverse_temp * total


def dot(a, b, dims, precision=highest):
    return lax.dot_general(a, b, dims, precision=precision, preferred_element_type=jnp.float32)


def split(x):
    high = x.astype(jnp.bfloat16)
    return high, (x - high.astype(jnp.float32)).astype(jnp.bfloat16)


def dot3(a, b, dims):
    return sum(
        lax.dot_general(x, y, dims, preferred_element_type=jnp.float32)
        for x, y in ((a[0], b[0]), (a[0], b[1]), (a[1], b[0]))
    )


def iota(shape, dim):
    return lax.broadcasted_iota(jnp.int32, shape, dim)


def matsubara(number):
    return (2.0 * number.astype(jnp.float32) + 1.0) * (math.pi / inverse_temp)


def spare_of(norb):
    used = norb * norb
    width = LANES - used
    pieces = -(-used // width)
    return used, width, pieces


def kept_rows(norb, rows):
    pieces = spare_of(norb)[2]
    extra = 0
    while pieces * (extra + 1) <= rows - (extra + 1):
        extra += 1
    return rows - extra


def pack(rows, norb):
    used, width, pieces = spare_of(norb)
    kept = kept_rows(norb, len(rows))
    out = list(rows[:kept])
    lane = iota(rows[0].shape, 1)
    for e, row in enumerate(rows[kept:]):
        for p in range(pieces):
            moved = pltpu.roll(row, (used - width * p) % LANES, 1)
            out[pieces * e + p] = jnp.where(lane < used, out[pieces * e + p], moved)
    return out


def unpack(kept, norb, rows):
    used, width, pieces = spare_of(norb)
    out = list(kept)
    lane = iota(kept[0].shape, 1)
    for e in range(rows - len(kept)):
        row = 0.0
        for p in range(pieces):
            moved = pltpu.roll(kept[pieces * e + p], (width * p - used) % LANES, 1)
            inside = (lane >= width * p) & (lane < min(width * (p + 1), used))
            row = jnp.where(inside, moved, row)
        out.append(row)
    return out


def spaced(ref, chips, norb, rows):
    pitch = kept_rows(norb, rows)
    return unpack([ref[pl.ds(r, chips, stride=pitch), :] for r in range(pitch)], norb, rows)


def upright(rows):
    return jnp.concatenate(rows, axis=0).T


def band_inside(shape, window_ref):
    band = iota(shape, 1)
    return (band >= window_ref[0, 0]) & (band < window_ref[0, 1])


def invert(mat_re, mat_im):
    size = len(mat_re)
    mat_re, mat_im = list(mat_re), list(mat_im)
    column = iota(mat_re[0].shape, 0)
    for p in range(size):
        at = column == p
        piv_re = mat_re[p][p : p + 1]
        piv_im = mat_im[p][p : p + 1]
        rec = 1.0 / (piv_re * piv_re + piv_im * piv_im)
        rec_re = piv_re * rec
        rec_im = -piv_im * rec
        old_re = jnp.where(at, 1.0, mat_re[p])
        old_im = jnp.where(at, 0.0, mat_im[p])
        row_re = old_re * rec_re - old_im * rec_im
        row_im = old_re * rec_im + old_im * rec_re
        for i in range(size):
            if i == p:
                continue
            col_re = mat_re[i][p : p + 1]
            col_im = mat_im[i][p : p + 1]
            rest_re = jnp.where(at, 0.0, mat_re[i])
            rest_im = jnp.where(at, 0.0, mat_im[i])
            mat_re[i] = rest_re - (col_re * row_re - col_im * row_im)
            mat_im[i] = rest_im - (col_re * row_im + col_im * row_re)
        mat_re[p] = row_re
        mat_im[p] = row_im
    return mat_re, mat_im


def rows_of(block, norb):
    return [block[norb * i : norb * (i + 1)] for i in range(norb)]


def project_kernel(
    norb, chips, freqs, core_axis, energy_ref, proj_ref, window_ref, packed_ref, plain_ref, flat_ref
):
    core = lax.axis_index(core_axis)
    for i in range(norb):
        flat_ref[2 * i : 2 * i + 2, :] = proj_ref[0, i]
    flat = jnp.where(band_inside(flat_ref.shape, window_ref), flat_ref[...], 0.0)
    pair = iota((LANES, 2 * norb), 0)
    orb = iota((LANES, 2 * norb), 1)
    first = sum((pair >= norb * t).astype(jnp.int32) for t in range(1, norb))
    second = pair - norb * first
    inside = pair < norb * norb
    picks = [
        jnp.where((2 * which + half == orb) & inside, 1.0, 0.0)
        for which in (first, second)
        for half in range(2)
    ]
    picked = dot(jnp.concatenate(picks, axis=0), flat, NN)
    i_re, i_im, j_re, j_im = (picked[LANES * k : LANES * (k + 1)] for k in range(4))
    pair_re = i_re * j_re + i_im * j_im
    pair_im = i_im * j_re - i_re * j_im
    energy = energy_ref[...]
    rows = freqs * chips
    row = iota((rows, energy.shape[1]), 0)
    place = row // chips
    lines = []
    for other in range(2):
        number = 2 * freqs * (row - chips * place) + freqs * (core ^ other) + place
        freq = matsubara(number)
        denom = 1.0 / (energy * energy + freq * freq)
        green_re = -energy * denom
        green_im = -freq * denom
        for left, right in ((green_re, -green_im), (green_im, green_re)):
            total = dot(left, pair_re, NT) + dot(right, pair_im, NT)
            at = rows * (len(lines) // freqs)
            plain_ref[at : at + rows, :] = total
            lines += [total[chips * f : chips * (f + 1)] for f in range(freqs)]
    lines = pack(lines, norb)
    for r, line in enumerate(lines):
        packed_ref[pl.ds(r, chips, stride=len(lines)), :] = line


def dyson_kernel(
    norb, chips, freqs, points, own_ref, sib_ref, sigma_ref, imp_ref, new_ref, tile_ref,
    mat_ref, sum_ref, small_ref, wide_ref, turn_ref,
):
    pairs = norb * norb
    group = 2 * freqs
    lines = spaced(own_ref, chips, norb, 2 * group)[:group]
    lines += spaced(sib_ref, chips, norb, 2 * group)[group:]
    for half in range(2):
        for part in range(2):
            at = group * part + freqs * half
            mat_ref[half, :, LANES * part : LANES * (part + 1)] = upright(lines[at : at + freqs])
    for which, ref in enumerate((sigma_ref, imp_ref)):
        for half in range(2):
            for i in range(norb):
                at = (which * 2 + half) * pairs + norb * i
                small_ref[at : at + norb, :] = ref[half, i]
    spread = jnp.where(iota((freqs, LANES), 1) // chips == iota((freqs, LANES), 0), 1.0, 0.0)
    wide_ref[...] = dot(small_ref[...], spread, NN)

    def rows(ref, base):
        return [ref[base + norb * i : base + norb * (i + 1), :] for i in range(norb)]

    sig_re, sig_im = rows(wide_ref, 0), rows(wide_ref, pairs)
    for part in range(2):
        lanes = pl.ds(LANES * part, LANES)
        mat = [
            [mat_ref[half, norb * i : norb * (i + 1), lanes] for i in range(norb)]
            for half in range(2)
        ]
        ainv_re, ainv_im = invert(*mat)
        gorb_re, gorb_im = invert(
            [a - s for a, s in zip(ainv_re, sig_re)], [a - s for a, s in zip(ainv_im, sig_im)]
        )
        for i in range(norb):
            sum_ref[norb * i : norb * (i + 1), lanes] = gorb_re[i]
            sum_ref[pairs + norb * i : pairs + norb * (i + 1), lanes] = gorb_im[i]
    both = sum_ref[:, :LANES] + sum_ref[:, LANES:]
    same = iota((LANES, LANES), 0) // chips == iota((LANES, LANES), 1) // chips
    sum_ref[:, :LANES] = dot(both, jnp.where(same, 1.0 / points, 0.0), NN)
    loc = [
        [sum_ref[base + norb * i : base + norb * (i + 1), :LANES] for i in range(norb)]
        for base in (0, pairs)
    ]
    inv = invert(*loc)
    imp = rows(wide_ref, 2 * pairs), rows(wide_ref, 3 * pairs)
    pitch = turn_ref.shape[1] // norb
    diff = [[v - m for v, m in zip(inv[half], imp[half])] for half in range(2)]
    for half in range(2):
        for i in range(norb):
            turn_ref[half, pitch * i : pitch * i + norb, :] = diff[half][i]
    mat_ref[...] = jnp.zeros_like(mat_ref)
    for half, sig, sign in ((0, sig_re, 1.0), (1, sig_im, -1.0)):
        for i in range(norb):
            across = turn_ref[half, pl.ds(i, norb, stride=pitch), :]
            fresh = sig[i] + 0.5 * (diff[half][i] + sign * across)
            mat_ref[half, norb * i : norb * (i + 1), :LANES] = fresh
    row = iota((group, LANES), 0)
    lane = iota((group, LANES), 1)
    tile = 0.0
    for half in range(2):
        choose = jnp.where(lane == chips * (row - freqs * half), 1.0, 0.0)
        tile = tile + dot(choose, mat_ref[half, :, :LANES], NT)
    for half in range(2):
        for i in range(norb):
            new_ref[half, i] = tile[freqs * half : freqs * (half + 1), norb * i : norb * (i + 1)]
    lines = pack([tile[r : r + 1] for r in range(group)], norb)
    for r, line in enumerate(lines):
        tile_ref[pl.ds(r, chips, stride=len(lines)), :] = jnp.broadcast_to(line, (chips, LANES))


def numbers(shape, chips, freqs, core):
    lane = iota(shape, 1)
    part = lane // LANES
    within = lane - LANES * part
    place = within // chips
    return 2 * freqs * (within - chips * place) + freqs * (core ^ part) + place


STEP = 16


def prepare_kernel(
    norb, chips, freqs, core_axis, energy_ref, proj_ref, window_ref, plain_ref,
    ainv_ref, green_ref, left_ref, side_ref, right_ref, flat_ref,
):
    core = lax.axis_index(core_axis)
    bands = energy_ref.shape[1]
    tall = green_ref.shape[1]
    count = green_ref.shape[2]
    rows = freqs * chips
    for part in range(2):
        mat = []
        for half in range(2):
            at = rows * (2 * part + half)
            turned = plain_ref[at : at + rows, :].T
            mat.append(rows_of(turned, norb))
        inv = invert(*mat)
        for half in range(2):
            for i in range(norb):
                ainv_ref[2 * half + part, norb * i : norb * (i + 1), :] = inv[half][i]

    flat_ref[...] = jnp.zeros_like(flat_ref)
    for i in range(norb):
        flat_ref[i : i + 1, :bands] = proj_ref[0, i, 0:1]
        flat_ref[STEP + i : STEP + i + 1, :bands] = proj_ref[0, i, 1:2]
    flat_ref[2 * STEP : 2 * STEP + 1, :bands] = energy_ref[...]
    keep = band_inside(flat_ref.shape, window_ref) | (iota(flat_ref.shape, 0) >= 2 * STEP)
    turned = jnp.where(keep, flat_ref[...], 0.0).T[:tall]
    energy = turned[:, 2 * STEP : 2 * STEP + 1]
    freq = matsubara(numbers((tall, count), chips, freqs, core))
    denom = 1.0 / (energy * energy + freq * freq)
    green_re = -energy * denom
    green_im = -freq * denom
    green_ref[0] = green_re
    green_ref[1] = green_im
    wide = 2 * STEP
    straight = turned[:, :wide]
    crossed = jnp.concatenate([turned[:, STEP:wide], turned[:, :STEP]], axis=1)
    early = iota(straight.shape, 1) < STEP
    left = jnp.concatenate([straight, jnp.where(early, -crossed, crossed)], axis=0)
    high, low = split(left)
    left_ref[...] = jnp.concatenate([high, high, low], axis=1)
    side_ref[:, :wide] = straight
    side_ref[:, wide:] = crossed
    for j in range(norb):
        p_re = turned[:, j : j + 1]
        p_im = turned[:, STEP + j : STEP + j + 1]
        re = split(green_re * p_re - green_im * p_im)
        im = split(green_re * p_im + green_im * p_re)
        for k in range(2):
            right_ref[j, :, 2 * count * k : 2 * count * k + count] = re[k]
            right_ref[j, :, 2 * count * k + count : 2 * count * (k + 1)] = im[k]


def solve(mat, rhs):
    size = len(mat[0])
    mat = [list(m) for m in mat]
    out = [list(r) for r in rhs]
    row = iota(mat[0][0].shape, 0)
    for p in range(size):
        at = row == p
        piv_re = mat[0][p][p : p + 1]
        piv_im = mat[1][p][p : p + 1]
        rec = 1.0 / (piv_re * piv_re + piv_im * piv_im)
        rec_re = piv_re * rec
        rec_im = -piv_im * rec
        old_re = jnp.where(at, -1.0, mat[0][p])
        old_im = jnp.where(at, 0.0, mat[1][p])
        col_re = old_re * rec_re - old_im * rec_im
        col_im = old_re * rec_im + old_im * rec_re
        for cols, start in ((mat, p + 1), (out, 0)):
            for q in range(start, size):
                x_re = cols[0][q][p : p + 1]
                x_im = cols[1][q][p : p + 1]
                rest_re = jnp.where(at, 0.0, cols[0][q])
                rest_im = jnp.where(at, 0.0, cols[1][q])
                cols[0][q] = rest_re - (col_re * x_re - col_im * x_im)
                cols[1][q] = rest_im - (col_re * x_im + col_im * x_re)
    return out


def density_kernel(
    norb, chips, freqs, core_axis, ainv_ref, green_ref, left_ref, side_ref, right_ref, own_ref, sib_ref,
    out_ref, sig_ref, vert_ref, sums_ref, held_ref, done,
):
    core = lax.axis_index(core_axis)
    fetch = pltpu.make_async_copy(right_ref, held_ref, done)
    fetch.start()
    group = 2 * freqs
    bands = out_ref.shape[2]
    tall = green_ref.shape[1]
    count = green_ref.shape[2]
    wide = 2 * STEP
    for part in range(2):
        lines = spaced((own_ref, sib_ref)[part], chips, norb, group)
        for half in range(2):
            sig_ref[2 * half + part] = upright(lines[freqs * half : freqs * (half + 1)])

    def columns(ref, half, part):
        return [ref[2 * half + part, pl.ds(j, norb, stride=norb), :] for j in range(norb)]

    spare = jnp.zeros((STEP - norb, norb * count), jnp.float32)
    vert_ref[norb:STEP] = spare
    vert_ref[STEP + norb : wide] = spare
    for part in range(2):
        sig = [columns(sig_ref, half, part) for half in range(2)]
        mat = [
            [a - s for a, s in zip(columns(ainv_ref, half, part), sig[half])] for half in range(2)
        ]
        turned = solve(mat, sig)
        for j in range(norb):
            sum_re, sum_im = sig[0][j], sig[1][j]
            for k in range(norb):
                y_re = turned[0][j][k : k + 1]
                y_im = turned[1][j][k : k + 1]
                sum_re = sum_re + (sig[0][k] * y_re - sig[1][k] * y_im)
                sum_im = sum_im + (sig[0][k] * y_im + sig[1][k] * y_re)
            spot = pl.ds(count * j + LANES * part, LANES)
            vert_ref[0:norb, spot] = sum_re
            vert_ref[STEP : STEP + norb, spot] = sum_im

    last = numbers((norb, count), chips, freqs, core) == count - 1
    orb = iota((norb, LANES), 1)
    ends = []
    for half in range(2):
        end = jnp.zeros((norb, LANES), jnp.float32)
        for j in range(norb):
            for part in range(2):
                spot = last[:, LANES * part : LANES * (part + 1)]
                entry = jnp.where(spot, columns(sig_ref, half, part)[j], 0.0)
                end = end + jnp.where(orb == j, jnp.sum(entry, axis=1, keepdims=True), 0.0)
        ends += [end, jnp.zeros((STEP - norb, LANES), jnp.float32)]
    left = left_ref[...]

    def mixed(block):
        high, low = split(block)
        stacked = jnp.concatenate([high, low, high], axis=0)
        return lax.dot_general(left, stacked, NN, preferred_element_type=jnp.float32)

    def join(re, im, right):
        re, im = split(re), split(im)
        top = [jnp.concatenate([re[k], -im[k]], axis=1) for k in range(2)]
        low = [jnp.concatenate([im[k], re[k]], axis=1) for k in range(2)]
        line = [jnp.concatenate([t, b], axis=0) for t, b in zip(top, low)]
        return dot3(line, right, NT)

    weight = -0.5 * inverse_temp * tail_weight(count)
    tail = weight * mixed(jnp.concatenate(ends, axis=0))
    side = side_ref[...]
    orbs = jnp.zeros((tall, LANES - STEP), jnp.float32)
    right = split(jnp.concatenate([side[:, :STEP], orbs, side[:, wide : wide + STEP], orbs], axis=1))
    total = join(tail[:tall], tail[tall:], right)
    fetch.wait()
    for j in range(norb):
        mix = mixed(vert_ref[:, count * j : count * (j + 1)])
        mix_re, mix_im = mix[:tall], mix[tall:]
        side_re = mix_re * green_ref[0] - mix_im * green_ref[1]
        side_im = mix_re * green_ref[1] + mix_im * green_ref[0]
        right = [held_ref[j, :, 2 * count * k : 2 * count * (k + 1)] for k in range(2)]
        total = total + join(side_re, side_im, right)
    sums_ref[...] = jnp.zeros_like(sums_ref)
    for half, sign in ((0, 1.0), (1, -1.0)):
        sums_ref[:tall, :tall] = total[tall * half : tall * (half + 1)]
        both = sums_ref[...] + sign * sums_ref[...].T
        out_ref[0, half] = both[:bands, :bands] / inverse_temp


BLOCK = pl.BlockSpec()
VMEM = pl.BlockSpec(memory_space=pltpu.VMEM)
SMEM = pl.BlockSpec(memory_space=pltpu.SMEM)


def struct(*shape, dtype=jnp.float32):
    return jax.ShapeDtypeStruct(shape, dtype)


def scratch(*shape):
    return pltpu.VMEM(shape, jnp.float32)


def run(body, out, specs, scratches=()):
    return pl.pallas_call(
        body,
        out_shape=out,
        in_specs=specs,
        out_specs=jax.tree.map(lambda _: VMEM, out),
        scratch_shapes=scratches,
        compiler_params=pltpu.CompilerParams(vmem_limit_bytes=32 * 1024 * 1024),
    )


def kernels(norb, bands, freqs, chips, cores, points):
    group = 2 * freqs
    pairs = norb * norb
    count = freqs * chips * cores
    wide = -(-bands // LANES) * LANES
    tall = -(-bands // 16) * 16
    long = kept_rows(norb, 2 * group)
    short = kept_rows(norb, group)
    axis = "core"

    def project(*refs):
        project_kernel(norb, chips, freqs, axis, *refs)

    def dyson(*refs):
        dyson_kernel(norb, chips, freqs, points, *refs)

    def prepare(*refs):
        prepare_kernel(norb, chips, freqs, axis, *refs)

    def rebuild(*refs):
        density_kernel(norb, chips, freqs, axis, *refs)

    first = run(
        project,
        (struct(chips * long, LANES), struct(2 * count, LANES)),
        [BLOCK, BLOCK, SMEM],
        [scratch(2 * norb, bands)],
    )
    second = run(
        dyson,
        (struct(2, norb, freqs, norb), struct(chips * short, LANES)),
        [VMEM] * 4,
        [
            scratch(2, LANES, 2 * LANES),
            scratch(2 * pairs, 2 * LANES),
            scratch(4 * pairs, freqs),
            scratch(4 * pairs, LANES),
            scratch(2, 16 * norb, LANES),
        ],
    )
    aside = run(
        prepare,
        (
            struct(4, pairs, LANES),
            struct(2, tall, count),
            struct(2 * tall, 6 * STEP, dtype=jnp.bfloat16),
            struct(tall, 4 * STEP),
            struct(norb, tall, 4 * count, dtype=jnp.bfloat16),
        ),
        [BLOCK, BLOCK, SMEM, VMEM],
        [scratch(LANES, wide)],
    )
    third = run(
        rebuild,
        struct(1, 2, bands, bands),
        [VMEM] * 4 + [pl.BlockSpec(memory_space=pl.ANY)] + [VMEM] * 2,
        [
            scratch(4, LANES, LANES),
            scratch(2 * STEP, norb * count),
            scratch(wide, wide),
            pltpu.VMEM((norb, tall, 4 * count), jnp.bfloat16),
            pltpu.SemaphoreType.DMA(()),
        ],
    )
    return first, aside, second, third


def local(energies, proj, window, sigma, impurity_inverse):
    norb, bands = proj.shape[2:]
    freqs = sigma.shape[3]
    chips = lax.axis_size("z")
    cores = lax.axis_size("core")
    points = energies.shape[0] * chips * cores
    first, aside, second, third = kernels(norb, bands, freqs, chips, cores, points)
    swap = [(0, 1), (1, 0)]
    proj = jnp.swapaxes(proj, 1, 2)

    def across(rows):
        got = lax.all_to_all(rows.reshape(chips, 1, -1), "z", 0, 0, tiled=True)
        return got.reshape(rows.shape)

    packed, plain = first(energies, proj, window)
    ready = aside(energies, proj, window, plain)
    got, ready = lax.optimization_barrier((across(packed), ready))
    sigma_new, tiles = second(got, lax.ppermute(got, "core", swap), sigma, impurity_inverse)
    back = across(tiles)
    density = third(*ready, back, lax.ppermute(back, "core", swap))
    return density, jnp.swapaxes(sigma_new, 2, 3)


def solution(mesh):
    parts, line = mesh.shape["parts"], mesh.shape["ka"]
    torus = Mesh(mesh.devices.reshape(parts, line // 2, 2), ("parts", "z", "core"))
    every = ("parts", "z", "core")
    line = ("z", "core")
    in_specs = (
        P(every, None),
        P(every, None, None, None),
        P(every, None),
        P("parts", None, None, line),
        P("parts", None, None, line),
    )
    out_specs = (P(every, None, None, None), P("parts", None, None, line))
    return jax.shard_map(local, mesh=torus, in_specs=in_specs, out_specs=out_specs, check_vma=False)
```

time: 130 us -> 133 us (1.023)
  blocking collectives: 107 us -> 32.4 us
  starting transfers between devices: 4.42 us -> 37.4 us
  waiting for transfers between devices: 0.66 us -> 30.7 us
  local copies, waits for them, and re-layouts: 2.08 us -> 10.3 us
  Pallas kernels: 15.2 us -> 20.5 us
    all_to_all x2 -> x1, blocking collectives: 107 us -> 32.4 us  [across(): got = lax.all_to_all(rows.reshape(chips, 1, -1), 'z', 0, 0, tiled=True)]
    all_to_all x0 -> x1, starting transfers between devices: none -> 33.2 us  [across(): got = lax.all_to_all(rows.reshape(chips, 1, -1), 'z', 0, 0, tiled=True)]
    all_to_all x0 -> x1, waiting for transfers between devices: none -> 29.7 us  [across(): got = lax.all_to_all(rows.reshape(chips, 1, -1), 'z', 0, 0, tiled=True)]
    unnamed x12 -> x18, local copies, waits for them, and re-layouts: 2.07 us -> 10.3 us
    pallas_call x3 -> x4, Pallas kernels: 15.2 us -> 20.5 us  [the longest x1 11.1 us: local(): density = third(*ready, back, lax.ppermute(back, 'core', swap))]
  transfers between devices with their start and end apart: 2 -> 3, of which waited for: 2 -> 2; matrix products, arithmetic and copies ran while one was open for 1% -> 2% of each run, Pallas kernels for 0% -> 2%
where the time goes in v1:
time: 133 us; the launch traced here: 132 us
  starting transfers between devices  37.4 us (28%)
  blocking collectives  32.4 us (24%)
  waiting for transfers between devices  30.7 us (23%)
  Pallas kernels  20.5 us (15%)
  local copies, waits for them, and re-layouts  10.3 us (8%)
    all_to_all x1, starting transfers between devices, across(): got = lax.all_to_all(rows.reshape(chips, 1, -1), 'z', 0, 0, tiled=True)  33.2 us
    all_to_all x1, blocking collectives, across(): got = lax.all_to_all(rows.reshape(chips, 1, -1), 'z', 0, 0, tiled=True)  32.4 us
    all_to_all x1, waiting for transfers between devices, across(): got = lax.all_to_all(rows.reshape(chips, 1, -1), 'z', 0, 0, tiled=True)  29.7 us
    pallas_call x1, Pallas kernels, local(): density = third(*ready, back, lax.ppermute(back, 'core', swap))  11.1 us
    unnamed x18, local copies, waits for them, and re-layouts  10.3 us
    pallas_call x1, Pallas kernels, local(): packed, plain = first(energies, proj, window)  3.73 us
    pallas_call x1, Pallas kernels, local(): second(got, lax.ppermute(got, 'core', swap), sigma, impurity_inverse)  3.28 us
  transfers between devices with their start and end apart: 3, of which 2 were waited for; matrix products, arithmetic and copies ran while one was open for 2% of the time, Pallas kernels for 2%

profile of v1, /device:TPU:37, one launch (start us, length us, event | category | flops | bytes accessed | tf_op | source)
XLA Modules:
  0.0 132.1 jit_solution(3828831959885894399)
XLA Ops:
  0.6 0.0 copy-start.2
  0.6 0.7 copy-done.2
  1.4 0.7 copy-done.4
  2.0 0.7 copy-done.6
  2.7 3.7 %shard_map.68 = (f32[416,128]{1,0:T(8,128)}, f32[512,128]{1,0:T(8,128)S(1)}) custom-call(f32[1,200]{1,0:T(1,128)S(1)} %copy-done.4, f32[1,10,2,200]{3,2,1,0:T(2,128)S(1)} %bitcast.11, s32[1,2]{1,0:T(1,128)S(1)} %copy-done.6), custom_call_target="tpu_custom_call" | custom-call | tf_op jit(solution)/shard_map/pallas_call | solution.py:532
  6.4 33.2 %all-to-all-start = ((f32[32,1,1664]{2,1,0:T(1,128)}), f32[32,1,1664]{2,1,0:T(1,128)S(1)}, u32[]{:S(2)}, u32[]{:S(2)}) async-start(f32[32,1,1664]{2,1,0:T(1,128)} %bitcast.1), calls=%async_computation | async-start | bytes 425984 | tf_op jit(solution)/shard_map/all_to_all | solution.py:529
  39.6 0.0 copy-start.3
  39.6 0.7 copy-done.3
  40.4 0.7 copy-done.5
  41.0 0.7 copy-done.7
  41.7 2.5 %shard_map.69 = (f32[4,100,128]{2,1,0:T(8,128)S(1)}, f32[2,208,256]{2,1,0:T(8,128)S(1)}, bf16[416,96]{1,0:T(8,128)(2,1)S(1)}, f32[208,64]{1,0:T(8,128)S(1)}, bf16[10,208,1024]{2,1,0:T(8,128)(2,1)S(1)}) custom-call(f32[1,200]{1,0:T(1,128)S(1)} %copy-done.5, f32[1,10,2,200]{3,2,1,0:T(2,128)S(1)} %bitcast.12, s32[1,2]{1,0:T(1,128)S(1)} %copy-done.7, ...), custom_call_target="tpu_custom_call" | custom-call | tf_op jit(solution)/shard_map/pallas_call | solution.py:533
  44.2 0.0 copy-start
  44.2 2.0 %copy-done = bf16[10,208,1024]{2,1,0:T(8,128)(2,1)} copy-done((bf16[10,208,1024]{2,1,0:T(8,128)(2,1)}, bf16[10,208,1024]{2,1,0:T(8,128)(2,1)S(1)}, u32[]{:S(2)}) %copy-start) | copy-done | bytes 4259864
  46.1 29.7 %all-to-all-done = f32[32,1,1664]{2,1,0:T(1,128)S(1)} async-done(((f32[32,1,1664]{2,1,0:T(1,128)}), f32[32,1,1664]{2,1,0:T(1,128)S(1)}, u32[]{:S(2)}, u32[]{:S(2)}) %all-to-all-start) | async-done | bytes 213024 | tf_op jit(solution)/shard_map/all_to_all | solution.py:529
  75.8 2.4 %collective-permute-start = (f32[416,128]{1,0:T(8,128)S(1)}, f32[416,128]{1,0:T(8,128)S(1)}, u32[]{:S(2)}, u32[]{:S(2)}) collective-permute-start(f32[416,128]{1,0:T(8,128)S(1)} %bitcast.6), channel_id=1, source_target_pairs={{0,1},{1,0},{2,3},{3,2},{4,5},{5,4},{6,7},{7,6},{8,9},{9,8},{10,11... | collective-permute-start | bytes 638984 | tf_op jit(solution)/shard_map/ppermute | solution.py:535
  78.2 1.0 copy.10.refs_2_
  79.3 1.0 copy.11.refs_3_
  80.3 0.0 collective-permute-done.refs_1_
  80.3 3.3 %shard_map.70 = (f32[2,10,4,10]{3,2,1,0:T(4,128)}, f32[224,128]{1,0:T(8,128)S(1)}) custom-call(f32[416,128]{1,0:T(8,128)S(1)} %bitcast.7, f32[416,128]{1,0:T(8,128)S(1)} %collective-permute-done.refs_1_, f32[2,10,10,4]{3,2,1,0:T(8,128)S(1)} %copy.10.refs_2_, f32[2,10,10,4]{3,2,1,0:T(8,128)S(1)} %copy.11.refs_3_), custom_call_target="tpu_custom_call" | custom-call | tf_op jit(solution)/shard_map/pallas_call | solution.py:535
  83.6 32.4 %all_to_all.10 = f32[32,1,896]{2,1,0:T(1,128)S(1)} all-to-all(f32[32,1,896]{2,1,0:T(1,128)S(1)} %bitcast.10), channel_id=1, replica_groups=mesh['parts'=4,'z'=32,'core'=2] {'z'}, dimensions={0} | all-to-all | bytes 229376 | tf_op jit(solution)/shard_map/all_to_all | solution.py:529
  115.9 1.8 %collective-permute-start.1 = (f32[224,128]{1,0:T(8,128)S(1)}, f32[224,128]{1,0:T(8,128)S(1)}, u32[]{:S(2)}, u32[]{:S(2)}) collective-permute-start(f32[224,128]{1,0:T(8,128)S(1)} %bitcast.8), channel_id=1, source_target_pairs={{0,1},{1,0},{2,3},{3,2},{4,5},{5,4},{6,7},{7,6},{8,9},{9,8},{10,11... | collective-permute-start | bytes 344072 | tf_op jit(solution)/shard_map/ppermute | solution.py:537
  117.7 1.0 collective-permute-done.1.refs_6_
  118.7 2.2 %copy-done.1 = bf16[10,208,1024]{2,1,0:T(8,128)(2,1)S(1)} copy-done((bf16[10,208,1024]{2,1,0:T(8,128)(2,1)S(1)}, bf16[10,208,1024]{2,1,0:T(8,128)(2,1)}, u32[]{:S(2)}) %copy-start.1) | copy-done | bytes 4259864
  120.9 11.1 %shard_map.71 = f32[1,2,200,200]{3,2,1,0:T(8,128)} custom-call(f32[4,100,128]{2,1,0:T(8,128)S(1)} %get-tuple-element.24.refs_0_, f32[2,208,256]{2,1,0:T(8,128)S(1)} %get-tuple-element.25.refs_1_, bf16[416,96]{1,0:T(8,128)(2,1)S(1)} %get-tuple-element.26.refs_2_, f32[208,64]{1,0:T(8,128)S(1)} %get-tuple-element.27.refs_3_, ...), custom_call_target="tpu_custom_call" | custom-call | tf_op jit(solution)/shard_map/pallas_call | solution.py:537
  (5 shorter events, 0.0 us)
Async XLA Ops:
  0.6 0.7 copy-start.2
  1.4 0.7 copy-start.4
  2.0 0.7 copy-start.6
  6.4 69.4 %all-to-all-start = ((f32[32,1,1664]{2,1,0:T(1,128)}), f32[32,1,1664]{2,1,0:T(1,128)S(1)}, u32[]{:S(2)}, u32[]{:S(2)}) async-start(f32[32,1,1664]{2,1,0:T(1,128)} %bitcast.1), calls=%async_computation | async-start | bytes 425984 | tf_op jit(solution)/shard_map/all_to_all | solution.py:529
  39.6 0.7 copy-start.3
  40.4 0.7 copy-start.5
  41.0 0.7 copy-start.7
  44.2 2.0 %copy-start = (bf16[10,208,1024]{2,1,0:T(8,128)(2,1)}, bf16[10,208,1024]{2,1,0:T(8,128)(2,1)S(1)}, u32[]{:S(2)}) copy-start(bf16[10,208,1024]{2,1,0:T(8,128)(2,1)S(1)} %get-tuple-element.28.refs_4_) | copy-start | bytes 12779524
  75.8 4.4 %collective-permute-start = (f32[416,128]{1,0:T(8,128)S(1)}, f32[416,128]{1,0:T(8,128)S(1)}, u32[]{:S(2)}, u32[]{:S(2)}) collective-permute-start(f32[416,128]{1,0:T(8,128)S(1)} %bitcast.6), channel_id=1, source_target_pairs={{0,1},{1,0},{2,3},{3,2},{4,5},{5,4},{6,7},{7,6},{8,9},{9,8},{10,11... | collective-permute-start | bytes 638984 | tf_op jit(solution)/shard_map/ppermute | solution.py:535
  115.9 2.7 %collective-permute-start.1 = (f32[224,128]{1,0:T(8,128)S(1)}, f32[224,128]{1,0:T(8,128)S(1)}, u32[]{:S(2)}, u32[]{:S(2)}) collective-permute-start(f32[224,128]{1,0:T(8,128)S(1)} %bitcast.8), channel_id=1, source_target_pairs={{0,1},{1,0},{2,3},{3,2},{4,5},{5,4},{6,7},{7,6},{8,9},{9,8},{10,11... | collective-permute-start | bytes 344072 | tf_op jit(solution)/shard_map/ppermute | solution.py:537
  118.7 2.2 %copy-start.1 = (bf16[10,208,1024]{2,1,0:T(8,128)(2,1)S(1)}, bf16[10,208,1024]{2,1,0:T(8,128)(2,1)}, u32[]{:S(2)}) copy-start(bf16[10,208,1024]{2,1,0:T(8,128)(2,1)} %copy-done) | copy-start | bytes 12779524

commit v2 on v1

--- a/solution.py
+++ b/solution.py
@@ -94,11 +94,6 @@
 
 def upright(rows):
     return jnp.concatenate(rows, axis=0).T
-
-
-def band_inside(shape, window_ref):
-    band = iota(shape, 1)
-    return (band >= window_ref[0, 0]) & (band < window_ref[0, 1])
 
 
 def invert(mat_re, mat_im):
@@ -134,15 +129,36 @@
     return [block[norb * i : norb * (i + 1)] for i in range(norb)]
 
 
+def fetched(sources, targets, sems):
+    copies = [pltpu.make_async_copy(a, b, sems.at[k]) for k, (a, b) in enumerate(zip(sources, targets))]
+    for copy in copies:
+        copy.start()
+
+    def wait():
+        for copy in copies:
+            copy.wait()
+
+    return wait
+
+
+def band_inside(shape, window_ref):
+    band = iota(shape, 1)
+    return (band >= window_ref[:, 0:1]) & (band < window_ref[:, 1:2])
+
+
 def project_kernel(
-    norb, chips, freqs, core_axis, energy_ref, proj_ref, window_ref, packed_ref, plain_ref, flat_ref
+    norb, chips, freqs, core_axis, energy_in, proj_in, window_in, packed_ref, plain_ref,
+    energy_ref, proj_ref, window_ref, flat_ref, sems,
 ):
+    wait = fetched((energy_in, proj_in, window_in), (energy_ref, proj_ref, window_ref), sems)
     core = lax.axis_index(core_axis)
-    for i in range(norb):
-        flat_ref[2 * i : 2 * i + 2, :] = proj_ref[0, i]
-    flat = jnp.where(band_inside(flat_ref.shape, window_ref), flat_ref[...], 0.0)
-    pair = iota((LANES, 2 * norb), 0)
-    orb = iota((LANES, 2 * norb), 1)
+    bands = energy_ref.shape[1]
+    rows = freqs * chips
+    flat_ref[...] = jnp.zeros_like(flat_ref)
+    freq = matsubara(numbers_down((2 * rows, bands), chips, freqs, core))
+    square = freq * freq
+    pair = iota((flat_ref.shape[0], LANES), 1)
+    orb = iota((flat_ref.shape[0], LANES), 0)
     first = sum((pair >= norb * t).astype(jnp.int32) for t in range(1, norb))
     second = pair - norb * first
     inside = pair < norb * norb
@@ -151,23 +167,24 @@
         for which in (first, second)
         for half in range(2)
     ]
-    picked = dot(jnp.concatenate(picks, axis=0), flat, NN)
-    i_re, i_im, j_re, j_im = (picked[LANES * k : LANES * (k + 1)] for k in range(4))
-    pair_re = i_re * j_re + i_im * j_im
-    pair_im = i_im * j_re - i_re * j_im
+    picks = jnp.concatenate(picks, axis=1)
+    wait()
+    for i in range(norb):
+        flat_ref[2 * i : 2 * i + 2, :bands] = proj_ref[0, i]
+    flat = jnp.where(band_inside(flat_ref.shape, window_ref), flat_ref[...], 0.0)
+    picked = dot(flat, picks, (((0,), (0,)), ((), ())))
+    i_re, i_im, j_re, j_im = (picked[:, LANES * k : LANES * (k + 1)] for k in range(4))
+    pair_re = (i_re * j_re + i_im * j_im)[:bands]
+    pair_im = (i_im * j_re - i_re * j_im)[:bands]
     energy = energy_ref[...]
-    rows = freqs * chips
-    row = iota((rows, energy.shape[1]), 0)
-    place = row // chips
+    denom = 1.0 / (energy * energy + square)
+    both = dot(-energy * denom, jnp.concatenate([pair_re, pair_im], axis=1), NN) + dot(
+        freq * denom, jnp.concatenate([pair_im, -pair_re], axis=1), NN
+    )
     lines = []
     for other in range(2):
-        number = 2 * freqs * (row - chips * place) + freqs * (core ^ other) + place
-        freq = matsubara(number)
-        denom = 1.0 / (energy * energy + freq * freq)
-        green_re = -energy * denom
-        green_im = -freq * denom
-        for left, right in ((green_re, -green_im), (green_im, green_re)):
-            total = dot(left, pair_re, NT) + dot(right, pair_im, NT)
+        for half in range(2):
+            total = both[rows * other : rows * (other + 1), LANES * half : LANES * (half + 1)]
             at = rows * (len(lines) // freqs)
             plain_ref[at : at + rows, :] = total
             lines += [total[chips * f : chips * (f + 1)] for f in range(freqs)]
@@ -177,8 +194,8 @@
 
 
 def dyson_kernel(
-    norb, chips, freqs, points, own_ref, sib_ref, sigma_ref, imp_ref, new_ref, tile_ref,
-    mat_ref, sum_ref, small_ref, wide_ref, turn_ref,
+    norb, chips, freqs, points, own_ref, sib_ref, wide_ref, new_ref, tile_ref,
+    mat_ref, turn_ref,
 ):
     pairs = norb * norb
     group = 2 * freqs
@@ -188,14 +205,6 @@
         for part in range(2):
             at = group * part + freqs * half
             mat_ref[half, :, LANES * part : LANES * (part + 1)] = upright(lines[at : at + freqs])
-    for which, ref in enumerate((sigma_ref, imp_ref)):
-        for half in range(2):
-            for i in range(norb):
-                at = (which * 2 + half) * pairs + norb * i
-                small_ref[at : at + norb, :] = ref[half, i]
-    spread = jnp.where(iota((freqs, LANES), 1) // chips == iota((freqs, LANES), 0), 1.0, 0.0)
-    wide_ref[...] = dot(small_ref[...], spread, NN)
-
     def rows(ref, base):
         return [ref[base + norb * i : base + norb * (i + 1), :] for i in range(norb)]
 
@@ -210,17 +219,13 @@
         gorb_re, gorb_im = invert(
             [a - s for a, s in zip(ainv_re, sig_re)], [a - s for a, s in zip(ainv_im, sig_im)]
         )
-        for i in range(norb):
-            sum_ref[norb * i : norb * (i + 1), lanes] = gorb_re[i]
-            sum_ref[pairs + norb * i : pairs + norb * (i + 1), lanes] = gorb_im[i]
-    both = sum_ref[:, :LANES] + sum_ref[:, LANES:]
-    same = iota((LANES, LANES), 0) // chips == iota((LANES, LANES), 1) // chips
-    sum_ref[:, :LANES] = dot(both, jnp.where(same, 1.0 / points, 0.0), NN)
-    loc = [
-        [sum_ref[base + norb * i : base + norb * (i + 1), :LANES] for i in range(norb)]
-        for base in (0, pairs)
-    ]
-    inv = invert(*loc)
+        sums = [a + b for a, b in zip(sums, gorb_re + gorb_im)] if part else gorb_re + gorb_im
+    shift = chips // 2
+    while shift:
+        sums = [a + pltpu.roll(a, LANES - shift, 1) for a in sums]
+        shift //= 2
+    sums = [a * (1.0 / points) for a in sums]
+    inv = invert(sums[:norb], sums[norb:])
     imp = rows(wide_ref, 2 * pairs), rows(wide_ref, 3 * pairs)
     pitch = turn_ref.shape[1] // norb
     diff = [[v - m for v, m in zip(inv[half], imp[half])] for half in range(2)]
@@ -233,18 +238,25 @@
             across = turn_ref[half, pl.ds(i, norb, stride=pitch), :]
             fresh = sig[i] + 0.5 * (diff[half][i] + sign * across)
             mat_ref[half, norb * i : norb * (i + 1), :LANES] = fresh
-    row = iota((group, LANES), 0)
-    lane = iota((group, LANES), 1)
-    tile = 0.0
+    lines = []
     for half in range(2):
-        choose = jnp.where(lane == chips * (row - freqs * half), 1.0, 0.0)
-        tile = tile + dot(choose, mat_ref[half, :, :LANES], NT)
+        flipped = mat_ref[half, :, :LANES].T
+        lines += [flipped[chips * f : chips * f + 1] for f in range(freqs)]
+    tile = jnp.concatenate(lines, axis=0)
     for half in range(2):
         for i in range(norb):
             new_ref[half, i] = tile[freqs * half : freqs * (half + 1), norb * i : norb * (i + 1)]
-    lines = pack([tile[r : r + 1] for r in range(group)], norb)
+    lines = pack(lines, norb)
     for r, line in enumerate(lines):
         tile_ref[pl.ds(r, chips, stride=len(lines)), :] = jnp.broadcast_to(line, (chips, LANES))
+
+
+def numbers_down(shape, chips, freqs, core):
+    row = iota(shape, 0)
+    part = row // LANES
+    within = row - LANES * part
+    place = within // chips
+    return 2 * freqs * (within - chips * place) + freqs * (core ^ part) + place
 
 
 def numbers(shape, chips, freqs, core):
@@ -259,10 +271,20 @@
 
 
 def prepare_kernel(
-    norb, chips, freqs, core_axis, energy_ref, proj_ref, window_ref, plain_ref,
-    ainv_ref, green_ref, left_ref, side_ref, right_ref, flat_ref,
+    norb, chips, freqs, core_axis, energy_in, proj_in, window_in, sigma_ref, imp_ref, plain_ref,
+    ainv_ref, green_ref, left_ref, side_ref, right_ref, wide_ref,
+    energy_ref, proj_ref, window_ref, flat_ref, small_ref, sems,
 ):
+    wait = fetched((energy_in, proj_in, window_in), (energy_ref, proj_ref, window_ref), sems)
     core = lax.axis_index(core_axis)
+    pairs = norb * norb
+    for which, ref in enumerate((sigma_ref, imp_ref)):
+        for half in range(2):
+            for i in range(norb):
+                at = (which * 2 + half) * pairs + norb * i
+                small_ref[at : at + norb, :] = ref[half, i]
+    spread = jnp.where(iota((freqs, LANES), 1) // chips == iota((freqs, LANES), 0), 1.0, 0.0)
+    wide_ref[...] = dot(small_ref[...], spread, NN)
     bands = energy_ref.shape[1]
     tall = green_ref.shape[1]
     count = green_ref.shape[2]
@@ -279,6 +301,7 @@
                 ainv_ref[2 * half + part, norb * i : norb * (i + 1), :] = inv[half][i]
 
     flat_ref[...] = jnp.zeros_like(flat_ref)
+    wait()
     for i in range(norb):
         flat_ref[i : i + 1, :bands] = proj_ref[0, i, 0:1]
         flat_ref[STEP + i : STEP + i + 1, :bands] = proj_ref[0, i, 1:2]
@@ -294,21 +317,26 @@
     green_ref[1] = green_im
     wide = 2 * STEP
     straight = turned[:, :wide]
-    crossed = jnp.concatenate([turned[:, STEP:wide], turned[:, :STEP]], axis=1)
-    early = iota(straight.shape, 1) < STEP
-    left = jnp.concatenate([straight, jnp.where(early, -crossed, crossed)], axis=0)
-    high, low = split(left)
+    high, low = split(straight)
     left_ref[...] = jnp.concatenate([high, high, low], axis=1)
-    side_ref[:, :wide] = straight
-    side_ref[:, wide:] = crossed
+    flat = jnp.where(keep, flat_ref[...], 0.0)
+    span = flat.shape[1]
+    energy = flat[2 * STEP : 2 * STEP + 1]
+    freq = matsubara(numbers_down((count, span), chips, freqs, core))
+    denom = 1.0 / (energy * energy + freq * freq)
+    green_re = -energy * denom
+    green_im = -freq * denom
     for j in range(norb):
-        p_re = turned[:, j : j + 1]
-        p_im = turned[:, STEP + j : STEP + j + 1]
+        p_re = flat[j : j + 1]
+        p_im = flat[STEP + j : STEP + j + 1]
         re = split(green_re * p_re - green_im * p_im)
         im = split(green_re * p_im + green_im * p_re)
         for k in range(2):
-            right_ref[j, :, 2 * count * k : 2 * count * k + count] = re[k]
-            right_ref[j, :, 2 * count * k + count : 2 * count * (k + 1)] = im[k]
+            right_ref[j, k, :, :span] = re[k]
+            right_ref[j, k, :, span:] = im[k]
+    side_ref[...] = jnp.zeros_like(side_ref)
+    side_ref[:norb, :span] = flat[:norb]
+    side_ref[:norb, span:] = flat[STEP : STEP + norb]
 
 
 def solve(mat, rhs):
@@ -343,8 +371,11 @@
     out_ref, sig_ref, vert_ref, sums_ref, held_ref, done,
 ):
     core = lax.axis_index(core_axis)
-    fetch = pltpu.make_async_copy(right_ref, held_ref, done)
-    fetch.start()
+    fetches = [
+        pltpu.make_async_copy(right_ref.at[j], held_ref.at[j], done.at[j]) for j in range(norb)
+    ]
+    for fetch in fetches:
+        fetch.start()
     group = 2 * freqs
     bands = out_ref.shape[2]
     tall = green_ref.shape[1]
@@ -358,7 +389,7 @@
     def columns(ref, half, part):
         return [ref[2 * half + part, pl.ds(j, norb, stride=norb), :] for j in range(norb)]
 
-    spare = jnp.zeros((STEP - norb, norb * count), jnp.float32)
+    spare = jnp.zeros((STEP - norb, 2 * norb * count), jnp.float32)
     vert_ref[norb:STEP] = spare
     vert_ref[STEP + norb : wide] = spare
     for part in range(2):
@@ -374,9 +405,12 @@
                 y_im = turned[1][j][k : k + 1]
                 sum_re = sum_re + (sig[0][k] * y_re - sig[1][k] * y_im)
                 sum_im = sum_im + (sig[0][k] * y_im + sig[1][k] * y_re)
-            spot = pl.ds(count * j + LANES * part, LANES)
-            vert_ref[0:norb, spot] = sum_re
-            vert_ref[STEP : STEP + norb, spot] = sum_im
+            at = 2 * count * j + LANES * part
+            vert_ref[0:norb, at : at + LANES] = sum_re
+            vert_ref[STEP : STEP + norb, at : at + LANES] = sum_im
+            at += count
+            vert_ref[0:norb, at : at + LANES] = sum_im
+            vert_ref[STEP : STEP + norb, at : at + LANES] = -sum_re
 
     last = numbers((norb, count), chips, freqs, core) == count - 1
     orb = iota((norb, LANES), 1)
@@ -388,7 +422,11 @@
                 spot = last[:, LANES * part : LANES * (part + 1)]
                 entry = jnp.where(spot, columns(sig_ref, half, part)[j], 0.0)
                 end = end + jnp.where(orb == j, jnp.sum(entry, axis=1, keepdims=True), 0.0)
-        ends += [end, jnp.zeros((STEP - norb, LANES), jnp.float32)]
+        ends.append(end)
+    blank = jnp.zeros((STEP - norb, LANES), jnp.float32)
+    ends = [
+        jnp.concatenate([a, blank, b, blank], axis=0) for a, b in (ends, (ends[1], -ends[0]))
+    ]
     left = left_ref[...]
 
     def mixed(block):
@@ -397,36 +435,32 @@
         return lax.dot_general(left, stacked, NN, preferred_element_type=jnp.float32)
 
     def join(re, im, right):
-        re, im = split(re), split(im)
-        top = [jnp.concatenate([re[k], -im[k]], axis=1) for k in range(2)]
-        low = [jnp.concatenate([im[k], re[k]], axis=1) for k in range(2)]
-        line = [jnp.concatenate([t, b], axis=0) for t, b in zip(top, low)]
-        return dot3(line, right, NT)
+        size = right[0].shape[1] // 2
+        left = [jnp.concatenate([r, i], axis=1) for r, i in zip(split(re), split(im))]
+        turned = [jnp.concatenate([-h[:, size:], h[:, :size]], axis=1) for h in right]
+        return dot3(left, [jnp.concatenate([a, b], axis=0) for a, b in zip(right, turned)], NN)
 
     weight = -0.5 * inverse_temp * tail_weight(count)
-    tail = weight * mixed(jnp.concatenate(ends, axis=0))
-    side = side_ref[...]
-    orbs = jnp.zeros((tall, LANES - STEP), jnp.float32)
-    right = split(jnp.concatenate([side[:, :STEP], orbs, side[:, wide : wide + STEP], orbs], axis=1))
-    total = join(tail[:tall], tail[tall:], right)
-    fetch.wait()
+    tail = weight * mixed(jnp.concatenate(ends, axis=1))
+    total = join(tail[:, :LANES], tail[:, LANES:], split(side_ref[...]))
+    green_re, green_im = green_ref[0], green_ref[1]
     for j in range(norb):
-        mix = mixed(vert_ref[:, count * j : count * (j + 1)])
-        mix_re, mix_im = mix[:tall], mix[tall:]
-        side_re = mix_re * green_ref[0] - mix_im * green_ref[1]
-        side_im = mix_re * green_ref[1] + mix_im * green_ref[0]
-        right = [held_ref[j, :, 2 * count * k : 2 * count * (k + 1)] for k in range(2)]
-        total = total + join(side_re, side_im, right)
+        mix = mixed(vert_ref[:, 2 * count * j : 2 * count * (j + 1)])
+        mix_re, mix_im = mix[:, :count], mix[:, count:]
+        side_re = mix_re * green_re - mix_im * green_im
+        side_im = mix_re * green_im + mix_im * green_re
+        fetches[j].wait()
+        total = total + join(side_re, side_im, [held_ref[j, k] for k in range(2)])
+    span = sums_ref.shape[1]
     sums_ref[...] = jnp.zeros_like(sums_ref)
     for half, sign in ((0, 1.0), (1, -1.0)):
-        sums_ref[:tall, :tall] = total[tall * half : tall * (half + 1)]
+        sums_ref[:tall, :] = total[:, span * half : span * (half + 1)]
         both = sums_ref[...] + sign * sums_ref[...].T
         out_ref[0, half] = both[:bands, :bands] / inverse_temp
 
 
-BLOCK = pl.BlockSpec()
+HBM = pl.BlockSpec(memory_space=pltpu.HBM)
 VMEM = pl.BlockSpec(memory_space=pltpu.VMEM)
-SMEM = pl.BlockSpec(memory_space=pltpu.SMEM)
 
 
 def struct(*shape, dtype=jnp.float32):
@@ -470,46 +504,51 @@
     def rebuild(*refs):
         density_kernel(norb, chips, freqs, axis, *refs)
 
+    inputs = [
+        pltpu.VMEM((1, bands), jnp.float32),
+        pltpu.VMEM((1, norb, 2, bands), jnp.float32),
+        pltpu.VMEM((1, 2), jnp.int32),
+    ]
     first = run(
         project,
         (struct(chips * long, LANES), struct(2 * count, LANES)),
-        [BLOCK, BLOCK, SMEM],
-        [scratch(2 * norb, bands)],
+        [HBM] * 3,
+        [*inputs, scratch(24, wide), pltpu.SemaphoreType.DMA((3,))],
     )
     second = run(
         dyson,
         (struct(2, norb, freqs, norb), struct(chips * short, LANES)),
-        [VMEM] * 4,
-        [
-            scratch(2, LANES, 2 * LANES),
-            scratch(2 * pairs, 2 * LANES),
-            scratch(4 * pairs, freqs),
-            scratch(4 * pairs, LANES),
-            scratch(2, 16 * norb, LANES),
-        ],
+        [VMEM] * 3,
+        [scratch(2, LANES, 2 * LANES), scratch(2, 16 * norb, LANES)],
     )
     aside = run(
         prepare,
         (
             struct(4, pairs, LANES),
             struct(2, tall, count),
-            struct(2 * tall, 6 * STEP, dtype=jnp.bfloat16),
-            struct(tall, 4 * STEP),
-            struct(norb, tall, 4 * count, dtype=jnp.bfloat16),
+            struct(tall, 6 * STEP, dtype=jnp.bfloat16),
+            struct(LANES, 2 * wide),
+            struct(norb, 2, count, 2 * wide, dtype=jnp.bfloat16),
+            struct(4 * pairs, LANES),
         ),
-        [BLOCK, BLOCK, SMEM, VMEM],
-        [scratch(LANES, wide)],
+        [HBM] * 3 + [VMEM] * 3,
+        [
+            *inputs,
+            scratch(LANES, wide),
+            scratch(4 * pairs, freqs),
+            pltpu.SemaphoreType.DMA((3,)),
+        ],
     )
     third = run(
         rebuild,
         struct(1, 2, bands, bands),
-        [VMEM] * 4 + [pl.BlockSpec(memory_space=pl.ANY)] + [VMEM] * 2,
+        [VMEM] * 4 + [HBM] + [VMEM] * 2,
         [
             scratch(4, LANES, LANES),
-            scratch(2 * STEP, norb * count),
+            scratch(2 * STEP, 2 * norb * count),
             scratch(wide, wide),
-            pltpu.VMEM((norb, tall, 4 * count), jnp.bfloat16),
-            pltpu.SemaphoreType.DMA(()),
+            pltpu.VMEM((norb, 2, count, 2 * wide), jnp.bfloat16),
+            pltpu.SemaphoreType.DMA((norb,)),
         ],
     )
     return first, aside, second, third
@@ -529,11 +568,14 @@
         got = lax.all_to_all(rows.reshape(chips, 1, -1), "z", 0, 0, tiled=True)
         return got.reshape(rows.shape)
 
-    packed, plain = first(energies, proj, window)
-    ready = aside(energies, proj, window, plain)
+    far = [pltpu.with_memory_space_constraint(x, pltpu.HBM) for x in (energies, proj, window)]
+    packed, plain = first(*far)
+    ready = aside(*far, sigma, impurity_inverse, plain)
     got, ready = lax.optimization_barrier((across(packed), ready))
-    sigma_new, tiles = second(got, lax.ppermute(got, "core", swap), sigma, impurity_inverse)
+    *ready, spread = ready
+    sigma_new, tiles = second(got, lax.ppermute(got, "core", swap), spread)
     back = across(tiles)
+    ready[4] = pltpu.with_memory_space_constraint(ready[4], pltpu.HBM)
     density = third(*ready, back, lax.ppermute(back, "core", swap))
     return density, jnp.swapaxes(sigma_new, 2, 3)
 

time: 133 us -> 124 us (0.932)
  local copies, waits for them, and re-layouts: 10.3 us -> 4.32 us
  Pallas kernels: 20.5 us -> 18.2 us
    unnamed x18 -> x4, local copies, waits for them, and re-layouts: 10.3 us -> 4.32 us
    pallas_call x1, Pallas kernels: 11.1 us -> 8.7 us  [local(): density = third(*ready, back, lax.ppermute(back, 'core', swap))]
  transfers between devices with their start and end apart: 3 -> 3, of which waited for: 2 -> 3; matrix products, arithmetic and copies ran while one was open for 2% -> 2% of each run, Pallas kernels for 2% -> 3%
where the time goes in v2:
time: 124 us
  starting transfers between devices  37.6 us (30%)
  blocking collectives  32.1 us (26%)
  waiting for transfers between devices  30.7 us (25%)
  Pallas kernels  18.2 us (15%)
  local copies, waits for them, and re-layouts  4.32 us (3%)
    all_to_all x1, starting transfers between devices, across(): got = lax.all_to_all(rows.reshape(chips, 1, -1), 'z', 0, 0, tiled=True)  33.2 us
    all_to_all x1, blocking collectives, across(): got = lax.all_to_all(rows.reshape(chips, 1, -1), 'z', 0, 0, tiled=True)  32.1 us
    all_to_all x1, waiting for transfers between devices, across(): got = lax.all_to_all(rows.reshape(chips, 1, -1), 'z', 0, 0, tiled=True)  28.6 us
    pallas_call x1, Pallas kernels, local(): density = third(*ready, back, lax.ppermute(back, 'core', swap))  8.7 us
    unnamed x4, local copies, waits for them, and re-layouts  4.32 us
    pallas_call x1, Pallas kernels, local(): packed, plain = first(*far)  3.46 us
    pallas_call x1, Pallas kernels, local(): ready = aside(*far, sigma, impurity_inverse, plain)  3.24 us
    pallas_call x1, Pallas kernels, local(): sigma_new, tiles = second(got, lax.ppermute(got, 'core', swap), spread)  2.75 us
  transfers between devices with their start and end apart: 3, of which 3 were waited for; matrix products, arithmetic and copies ran while one was open for 2% of the time, Pallas kernels for 3%

profile of v2, /device:TPU:37, one launch (start us, length us, event | category | flops | bytes accessed | tf_op | source)
XLA Modules:
  0.0 123.8 jit_solution(16041338231972739303)
XLA Ops:
  0.6 3.5 %shard_map.68 = (f32[416,128]{1,0:T(8,128)}, f32[512,128]{1,0:T(8,128)S(1)}) custom-call(f32[1,200]{1,0:T(1,128)} %refs_0_.3, f32[1,10,2,200]{3,2,1,0:T(2,128)} %bitcast.11, s32[1,2]{1,0:T(1,128)} %refs_2_.3), custom_call_target="tpu_custom_call" | custom-call | tf_op jit(solution)/shard_map/pallas_call | solution.py:572
  4.1 33.2 %all-to-all-start = ((f32[32,1,1664]{2,1,0:T(1,128)}), f32[32,1,1664]{2,1,0:T(1,128)S(1)}, u32[]{:S(2)}, u32[]{:S(2)}) async-start(f32[32,1,1664]{2,1,0:T(1,128)} %bitcast.1), calls=%async_computation | async-start | bytes 425984 | tf_op jit(solution)/shard_map/all_to_all | solution.py:568
  37.3 1.0 copy.10.refs_3_
  38.3 1.0 copy.11.refs_4_
  39.3 3.2 %shard_map.69 = (f32[4,100,128]{2,1,0:T(8,128)S(1)}, f32[2,208,256]{2,1,0:T(8,128)S(1)}, bf16[208,96]{1,0:T(8,128)(2,1)S(1)}, f32[128,512]{1,0:T(8,128)S(1)}, bf...) custom-call(f32[1,200]{1,0:T(1,128)} %refs_0_.3, f32[1,10,2,200]{3,2,1,0:T(2,128)} %bitcast.12, ...), custom_call_target="tpu_custom_call" | custom-call | tf_op jit(solution)/shard_map/pallas_call | solution.py:573
  42.6 0.0 copy-start
  42.6 2.3 %copy-done = bf16[10,2,256,512]{3,2,1,0:T(8,128)(2,1)} copy-done((bf16[10,2,256,512]{3,2,1,0:T(8,128)(2,1)}, bf16[10,2,256,512]{3,2,1,0:T(8,128)(2,1)S(1)}, u32[]{:S(2)}) %copy-start) | copy-done | bytes 5242904
  44.9 28.6 %all-to-all-done = f32[32,1,1664]{2,1,0:T(1,128)S(1)} async-done(((f32[32,1,1664]{2,1,0:T(1,128)}), f32[32,1,1664]{2,1,0:T(1,128)S(1)}, u32[]{:S(2)}, u32[]{:S(2)}) %all-to-all-start) | async-done | bytes 213024 | tf_op jit(solution)/shard_map/all_to_all | solution.py:568
  73.5 2.4 %collective-permute-start = (f32[416,128]{1,0:T(8,128)S(1)}, f32[416,128]{1,0:T(8,128)S(1)}, u32[]{:S(2)}, u32[]{:S(2)}) collective-permute-start(f32[416,128]{1,0:T(8,128)S(1)} %bitcast.6), channel_id=1, source_target_pairs={{0,1},{1,0},{2,3},{3,2},{4,5},{5,4},{6,7},{7,6},{8,9},{9,8},{10,11... | collective-permute-start | bytes 638984 | tf_op jit(solution)/shard_map/ppermute | solution.py:576
  75.9 1.1 collective-permute-done.refs_1_
  77.0 2.8 %shard_map.70 = (f32[2,10,4,10]{3,2,1,0:T(4,128)}, f32[224,128]{1,0:T(8,128)S(1)}) custom-call(f32[416,128]{1,0:T(8,128)S(1)} %bitcast.7, f32[416,128]{1,0:T(8,128)S(1)} %collective-permute-done.refs_1_, f32[400,128]{1,0:T(8,128)S(1)} %get-tuple-element.33.refs_2_), custom_call_target="tpu_custom_call" | custom-call | tf_op jit(solution)/shard_map/pallas_call | solution.py:576
  79.8 32.1 %all_to_all.10 = f32[32,1,896]{2,1,0:T(1,128)S(1)} all-to-all(f32[32,1,896]{2,1,0:T(1,128)S(1)} %bitcast.10), channel_id=1, replica_groups=mesh['parts'=4,'z'=32,'core'=2] {'z'}, dimensions={0} | all-to-all | bytes 229376 | tf_op jit(solution)/shard_map/all_to_all | solution.py:568
  111.9 2.0 %collective-permute-start.1 = (f32[224,128]{1,0:T(8,128)S(1)}, f32[224,128]{1,0:T(8,128)S(1)}, u32[]{:S(2)}, u32[]{:S(2)}) collective-permute-start(f32[224,128]{1,0:T(8,128)S(1)} %bitcast.8), channel_id=1, source_target_pairs={{0,1},{1,0},{2,3},{3,2},{4,5},{5,4},{6,7},{7,6},{8,9},{9,8},{10,11... | collective-permute-start | bytes 344072 | tf_op jit(solution)/shard_map/ppermute | solution.py:579
  113.9 1.0 collective-permute-done.1.refs_6_
  114.9 8.7 %shard_map.71 = f32[1,2,200,200]{3,2,1,0:T(8,128)} custom-call(f32[4,100,128]{2,1,0:T(8,128)S(1)} %get-tuple-element.27.refs_0_, f32[2,208,256]{2,1,0:T(8,128)S(1)} %get-tuple-element.28.refs_1_, bf16[208,96]{1,0:T(8,128)(2,1)S(1)} %get-tuple-element.29.refs_2_, f32[128,512]{1,0:T(8,128)S(1)} %get-tuple-element.30.refs_3_, ...), custom_call_target="tpu_custom_call" | custom-call | tf_op jit(solution)/shard_map/pallas_call | solution.py:579
Async XLA Ops:
  4.1 69.4 %all-to-all-start = ((f32[32,1,1664]{2,1,0:T(1,128)}), f32[32,1,1664]{2,1,0:T(1,128)S(1)}, u32[]{:S(2)}, u32[]{:S(2)}) async-start(f32[32,1,1664]{2,1,0:T(1,128)} %bitcast.1), calls=%async_computation | async-start | bytes 425984 | tf_op jit(solution)/shard_map/all_to_all | solution.py:568
  42.6 2.3 %copy-start = (bf16[10,2,256,512]{3,2,1,0:T(8,128)(2,1)}, bf16[10,2,256,512]{3,2,1,0:T(8,128)(2,1)S(1)}, u32[]{:S(2)}) copy-start(bf16[10,2,256,512]{3,2,1,0:T(8,128)(2,1)S(1)} %get-tuple-element.31.refs_4_) | copy-start | bytes 15728644
  73.5 3.5 %collective-permute-start = (f32[416,128]{1,0:T(8,128)S(1)}, f32[416,128]{1,0:T(8,128)S(1)}, u32[]{:S(2)}, u32[]{:S(2)}) collective-permute-start(f32[416,128]{1,0:T(8,128)S(1)} %bitcast.6), channel_id=1, source_target_pairs={{0,1},{1,0},{2,3},{3,2},{4,5},{5,4},{6,7},{7,6},{8,9},{9,8},{10,11... | collective-permute-start | bytes 638984 | tf_op jit(solution)/shard_map/ppermute | solution.py:576
  111.9 3.0 %collective-permute-start.1 = (f32[224,128]{1,0:T(8,128)S(1)}, f32[224,128]{1,0:T(8,128)S(1)}, u32[]{:S(2)}, u32[]{:S(2)}) collective-permute-start(f32[224,128]{1,0:T(8,128)S(1)} %bitcast.8), channel_id=1, source_target_pairs={{0,1},{1,0},{2,3},{3,2},{4,5},{5,4},{6,7},{7,6},{8,9},{9,8},{10,11... | collective-permute-start | bytes 344072 | tf_op jit(solution)/shard_map/ppermute | solution.py:579

commit v3 on v2

--- a/solution.py
+++ b/solution.py
@@ -155,7 +155,7 @@
     bands = energy_ref.shape[1]
     rows = freqs * chips
     flat_ref[...] = jnp.zeros_like(flat_ref)
-    freq = matsubara(numbers_down((2 * rows, bands), chips, freqs, core))
+    freq = matsubara(numbers((2 * rows, bands), 0, chips, 1, freqs, core))
     square = freq * freq
     pair = iota((flat_ref.shape[0], LANES), 1)
     orb = iota((flat_ref.shape[0], LANES), 0)
@@ -248,30 +248,26 @@
             new_ref[half, i] = tile[freqs * half : freqs * (half + 1), norb * i : norb * (i + 1)]
     lines = pack(lines, norb)
     for r, line in enumerate(lines):
-        tile_ref[pl.ds(r, chips, stride=len(lines)), :] = jnp.broadcast_to(line, (chips, LANES))
-
-
-def numbers_down(shape, chips, freqs, core):
-    row = iota(shape, 0)
-    part = row // LANES
-    within = row - LANES * part
+        tile_ref[0, :, LANES * r : LANES * (r + 1)] = line
+
+
+def numbers(shape, dim, chips, near, freqs, core):
+    spot = iota(shape, dim)
+    part = spot // LANES
+    within = spot - LANES * part
     place = within // chips
-    return 2 * freqs * (within - chips * place) + freqs * (core ^ part) + place
-
-
-def numbers(shape, chips, freqs, core):
-    lane = iota(shape, 1)
-    part = lane // LANES
-    within = lane - LANES * part
-    place = within // chips
-    return 2 * freqs * (within - chips * place) + freqs * (core ^ part) + place
+    chip = within - chips * place
+    far = chips // near
+    close = chip // far
+    chip = near * (chip - far * close) + close
+    return 2 * freqs * chip + freqs * (core ^ part) + place
 
 
 STEP = 16
 
 
 def prepare_kernel(
-    norb, chips, freqs, core_axis, energy_in, proj_in, window_in, sigma_ref, imp_ref, plain_ref,
+    norb, chips, near, freqs, core_axis, energy_in, proj_in, window_in, sigma_ref, imp_ref, plain_ref,
     ainv_ref, green_ref, left_ref, side_ref, right_ref, wide_ref,
     energy_ref, proj_ref, window_ref, flat_ref, small_ref, sems,
 ):
@@ -293,8 +289,12 @@
         mat = []
         for half in range(2):
             at = rows * (2 * part + half)
-            turned = plain_ref[at : at + rows, :].T
-            mat.append(rows_of(turned, norb))
+            order = [
+                plain_ref[pl.ds(at + chips * f + close, chips // near, stride=near), :]
+                for f in range(freqs)
+                for close in range(near)
+            ]
+            mat.append(rows_of(upright(order), norb))
         inv = invert(*mat)
         for half in range(2):
             for i in range(norb):
@@ -309,7 +309,7 @@
     keep = band_inside(flat_ref.shape, window_ref) | (iota(flat_ref.shape, 0) >= 2 * STEP)
     turned = jnp.where(keep, flat_ref[...], 0.0).T[:tall]
     energy = turned[:, 2 * STEP : 2 * STEP + 1]
-    freq = matsubara(numbers((tall, count), chips, freqs, core))
+    freq = matsubara(numbers((tall, count), 1, chips, near, freqs, core))
     denom = 1.0 / (energy * energy + freq * freq)
     green_re = -energy * denom
     green_im = -freq * denom
@@ -322,7 +322,7 @@
     flat = jnp.where(keep, flat_ref[...], 0.0)
     span = flat.shape[1]
     energy = flat[2 * STEP : 2 * STEP + 1]
-    freq = matsubara(numbers_down((count, span), chips, freqs, core))
+    freq = matsubara(numbers((count, span), 0, chips, near, freqs, core))
     denom = 1.0 / (energy * energy + freq * freq)
     green_re = -energy * denom
     green_im = -freq * denom
@@ -367,7 +367,7 @@
 
 
 def density_kernel(
-    norb, chips, freqs, core_axis, ainv_ref, green_ref, left_ref, side_ref, right_ref, own_ref, sib_ref,
+    norb, chips, near, freqs, core_axis, ainv_ref, green_ref, left_ref, side_ref, right_ref, own_ref, sib_ref,
     out_ref, sig_ref, vert_ref, sums_ref, held_ref, done,
 ):
     core = lax.axis_index(core_axis)
@@ -412,7 +412,7 @@
             vert_ref[0:norb, at : at + LANES] = sum_im
             vert_ref[STEP : STEP + norb, at : at + LANES] = -sum_re
 
-    last = numbers((norb, count), chips, freqs, core) == count - 1
+    last = numbers((norb, count), 1, chips, near, freqs, core) == count - 1
     orb = iota((norb, LANES), 1)
     ends = []
     for half in range(2):
@@ -482,7 +482,7 @@
     )
 
 
-def kernels(norb, bands, freqs, chips, cores, points):
+def kernels(norb, bands, freqs, chips, near, cores, points):
     group = 2 * freqs
     pairs = norb * norb
     count = freqs * chips * cores
@@ -499,10 +499,10 @@
         dyson_kernel(norb, chips, freqs, points, *refs)
 
     def prepare(*refs):
-        prepare_kernel(norb, chips, freqs, axis, *refs)
+        prepare_kernel(norb, chips, near, freqs, axis, *refs)
 
     def rebuild(*refs):
-        density_kernel(norb, chips, freqs, axis, *refs)
+        density_kernel(norb, chips, near, freqs, axis, *refs)
 
     inputs = [
         pltpu.VMEM((1, bands), jnp.float32),
@@ -517,7 +517,7 @@
     )
     second = run(
         dyson,
-        (struct(2, norb, freqs, norb), struct(chips * short, LANES)),
+        (struct(2, norb, freqs, norb), struct(1, 1, short * LANES)),
         [VMEM] * 3,
         [scratch(2, LANES, 2 * LANES), scratch(2, 16 * norb, LANES)],
     )
@@ -557,15 +557,16 @@
 def local(energies, proj, window, sigma, impurity_inverse):
     norb, bands = proj.shape[2:]
     freqs = sigma.shape[3]
-    chips = lax.axis_size("z")
+    near = lax.axis_size("near")
+    chips = lax.axis_size("far") * near
     cores = lax.axis_size("core")
     points = energies.shape[0] * chips * cores
-    first, aside, second, third = kernels(norb, bands, freqs, chips, cores, points)
+    first, aside, second, third = kernels(norb, bands, freqs, chips, near, cores, points)
     swap = [(0, 1), (1, 0)]
     proj = jnp.swapaxes(proj, 1, 2)
 
     def across(rows):
-        got = lax.all_to_all(rows.reshape(chips, 1, -1), "z", 0, 0, tiled=True)
+        got = lax.all_to_all(rows.reshape(chips, 1, -1), ("far", "near"), 0, 0, tiled=True)
         return got.reshape(rows.shape)
 
     far = [pltpu.with_memory_space_constraint(x, pltpu.HBM) for x in (energies, proj, window)]
@@ -574,7 +575,8 @@
     got, ready = lax.optimization_barrier((across(packed), ready))
     *ready, spread = ready
     sigma_new, tiles = second(got, lax.ppermute(got, "core", swap), spread)
-    back = across(tiles)
+    back = lax.all_gather(tiles, "far", axis=0, tiled=True)
+    back = lax.all_gather(back, "near", axis=0, tiled=True).reshape(-1, LANES)
     ready[4] = pltpu.with_memory_space_constraint(ready[4], pltpu.HBM)
     density = third(*ready, back, lax.ppermute(back, "core", swap))
     return density, jnp.swapaxes(sigma_new, 2, 3)
@@ -582,9 +584,13 @@
 
 def solution(mesh):
     parts, line = mesh.shape["parts"], mesh.shape["ka"]
-    torus = Mesh(mesh.devices.reshape(parts, line // 2, 2), ("parts", "z", "core"))
-    every = ("parts", "z", "core")
-    line = ("z", "core")
+    near = 4
+    chips = line // 2
+    torus = Mesh(
+        mesh.devices.reshape(parts, chips // near, near, 2), ("parts", "far", "near", "core")
+    )
+    every = ("parts", "far", "near", "core")
+    line = ("far", "near", "core")
     in_specs = (
         P(every, None),
         P(every, None, None, None),

time: 124 us -> 139 us (1.12)
  blocking collectives: 32.1 us -> 39.9 us
  starting transfers between devices: 37.6 us -> 45 us
    all_gather x0 -> x2, blocking collectives: none -> 39.9 us  [the longest x1 29.2 us: local(): back = lax.all_gather(tiles, 'far', axis=0, tiled=True)]
    all_to_all x1 -> x0, blocking collectives: 32.1 us -> none  [across(): got = lax.all_to_all(rows.reshape(chips, 1, -1), 'z', 0, 0, tiled=True)]
    ppermute x1, starting transfers between devices: 2.02 us -> 9.41 us  [local(): density = third(*ready, back, lax.ppermute(back, 'core', swap))]
  transfers between devices with their start and end apart: 3 -> 3, of which waited for: 3 -> 3; matrix products, arithmetic and copies ran while one was open for 2% -> 1% of each run, Pallas kernels for 3% -> 2%
where the time goes in v3:
time: 139 us
  starting transfers between devices  45 us (32%)
  blocking collectives  39.9 us (29%)
  waiting for transfers between devices  30.6 us (22%)
  Pallas kernels  18.3 us (13%)
  local copies, waits for them, and re-layouts  4.32 us (3%)
    all_to_all x1, starting transfers between devices, across(): lax.all_to_all(rows.reshape(chips, 1, -1), ('far', 'near'), 0, 0, tiled=T...  33.2 us
    all_gather x1, blocking collectives, local(): back = lax.all_gather(tiles, 'far', axis=0, tiled=True)  29.2 us
    all_to_all x1, waiting for transfers between devices, across(): lax.all_to_all(rows.reshape(chips, 1, -1), ('far', 'near'), 0, 0, tiled=T...  28.5 us
    all_gather x1, blocking collectives, local(): back = lax.all_gather(back, 'near', axis=0, tiled=True).reshape(-1, LANES)  10.7 us
    ppermute x1, starting transfers between devices, local(): density = third(*ready, back, lax.ppermute(back, 'core', swap))  9.41 us
    pallas_call x1, Pallas kernels, local(): density = third(*ready, back, lax.ppermute(back, 'core', swap))  8.7 us
    unnamed x4, local copies, waits for them, and re-layouts  4.32 us
    pallas_call x1, Pallas kernels, local(): packed, plain = first(*far)  3.46 us
  transfers between devices with their start and end apart: 3, of which 3 were waited for; matrix products, arithmetic and copies ran while one was open for 1% of the time, Pallas kernels for 2%

profile of v3, /device:TPU:37, one launch (start us, length us, event | category | flops | bytes accessed | tf_op | source)
XLA Modules:
  0.0 138.9 jit_solution(1379529852411902688)
XLA Ops:
  0.6 3.5 %shard_map.68 = (f32[416,128]{1,0:T(8,128)}, f32[512,128]{1,0:T(8,128)S(1)}) custom-call(f32[1,200]{1,0:T(1,128)} %refs_0_.3, f32[1,10,2,200]{3,2,1,0:T(2,128)} %bitcast.9, s32[1,2]{1,0:T(1,128)} %refs_2_.3), custom_call_target="tpu_custom_call" | custom-call | tf_op jit(solution)/shard_map/pallas_call | solution.py:573
  4.1 33.2 %all-to-all-start = ((f32[32,1,1664]{2,1,0:T(1,128)}), f32[32,1,1664]{2,1,0:T(1,128)S(1)}, u32[]{:S(2)}, u32[]{:S(2)}) async-start(f32[32,1,1664]{2,1,0:T(1,128)} %bitcast.1), calls=%async_computation | async-start | bytes 425984 | tf_op jit(solution)/shard_map/all_to_all | solution.py:569
  37.3 1.0 copy.10.refs_3_
  38.3 1.0 copy.11.refs_4_
  39.3 3.4 %shard_map.69 = (f32[4,100,128]{2,1,0:T(8,128)S(1)}, f32[2,208,256]{2,1,0:T(8,128)S(1)}, bf16[208,96]{1,0:T(8,128)(2,1)S(1)}, f32[128,512]{1,0:T(8,128)S(1)}, bf...) custom-call(f32[1,200]{1,0:T(1,128)} %refs_0_.3, f32[1,10,2,200]{3,2,1,0:T(2,128)} %bitcast.10, ...), custom_call_target="tpu_custom_call" | custom-call | tf_op jit(solution)/shard_map/pallas_call | solution.py:574
  42.7 0.0 copy-start
  42.7 2.3 %copy-done = bf16[10,2,256,512]{3,2,1,0:T(8,128)(2,1)} copy-done((bf16[10,2,256,512]{3,2,1,0:T(8,128)(2,1)}, bf16[10,2,256,512]{3,2,1,0:T(8,128)(2,1)S(1)}, u32[]{:S(2)}) %copy-start) | copy-done | bytes 5242904
  45.0 28.5 %all-to-all-done = f32[32,1,1664]{2,1,0:T(1,128)S(1)} async-done(((f32[32,1,1664]{2,1,0:T(1,128)}), f32[32,1,1664]{2,1,0:T(1,128)S(1)}, u32[]{:S(2)}, u32[]{:S(2)}) %all-to-all-start) | async-done | bytes 213024 | tf_op jit(solution)/shard_map/all_to_all | solution.py:569
  73.5 2.4 %collective-permute-start = (f32[416,128]{1,0:T(8,128)S(1)}, f32[416,128]{1,0:T(8,128)S(1)}, u32[]{:S(2)}, u32[]{:S(2)}) collective-permute-start(f32[416,128]{1,0:T(8,128)S(1)} %bitcast.5), channel_id=1, source_target_pairs={{0,1},{1,0},{2,3},{3,2},{4,5},{5,4},{6,7},{7,6},{8,9},{9,8},{10,11... | collective-permute-start | bytes 638984 | tf_op jit(solution)/shard_map/ppermute | solution.py:577
  75.9 1.1 collective-permute-done.refs_1_
  77.0 2.7 %shard_map.70 = (f32[2,10,4,10]{3,2,1,0:T(4,128)}, f32[1,1,896]{2,1,0:T(1,128)S(1)}) custom-call(f32[416,128]{1,0:T(8,128)S(1)} %bitcast.6, f32[416,128]{1,0:T(8,128)S(1)} %collective-permute-done.refs_1_, f32[400,128]{1,0:T(8,128)S(1)} %get-tuple-element.33.refs_2_), custom_call_target="tpu_custom_call" | custom-call | tf_op jit(solution)/shard_map/pallas_call | solution.py:577
  79.8 29.2 %all_gather.6 = f32[8,1,896]{2,1,0:T(1,128)S(1)} all-gather(f32[1,1,896]{2,1,0:T(1,128)S(1)} %get-tuple-element.34), channel_id=1, replica_groups=mesh['parts'=4,'far'=8,'near'=4,'core'=2] {'far'}, dimensions={0}, use_global_device_ids=true | all-gather | bytes 32256 | tf_op jit(solution)/shard_map/all_gather | solution.py:578
  108.9 10.7 %all_gather.7 = f32[32,1,896]{2,1,0:T(1,128)S(1)} all-gather(f32[8,1,896]{2,1,0:T(1,128)S(1)} %all_gather.6), channel_id=1, replica_groups=mesh['parts'=4,'far'=8,'near'=4,'core'=2] {'near'}, dimensions={0}, use_global_device_ids=true | all-gather | bytes 143360 | tf_op jit(solution)/shard_map/all_gather | solution.py:579
  119.7 9.4 %collective-permute-start.1 = (f32[224,128]{1,0:T(8,128)S(1)}, f32[224,128]{1,0:T(8,128)S(1)}, u32[]{:S(2)}, u32[]{:S(2)}) collective-permute-start(f32[224,128]{1,0:T(8,128)S(1)} %bitcast.7), channel_id=1, source_target_pairs={{0,1},{1,0},{2,3},{3,2},{4,5},{5,4},{6,7},{7,6},{8,9},{9,8},{10,11... | collective-permute-start | bytes 344072 | tf_op jit(solution)/shard_map/ppermute | solution.py:581
  129.1 1.0 collective-permute-done.1.refs_6_
  130.0 8.7 %shard_map.71 = f32[1,2,200,200]{3,2,1,0:T(8,128)} custom-call(f32[4,100,128]{2,1,0:T(8,128)S(1)} %get-tuple-element.27.refs_0_, f32[2,208,256]{2,1,0:T(8,128)S(1)} %get-tuple-element.28.refs_1_, bf16[208,96]{1,0:T(8,128)(2,1)S(1)} %get-tuple-element.29.refs_2_, f32[128,512]{1,0:T(8,128)S(1)} %get-tuple-element.30.refs_3_, ...), custom_call_target="tpu_custom_call" | custom-call | tf_op jit(solution)/shard_map/pallas_call | solution.py:581
Async XLA Ops:
  4.1 69.4 %all-to-all-start = ((f32[32,1,1664]{2,1,0:T(1,128)}), f32[32,1,1664]{2,1,0:T(1,128)S(1)}, u32[]{:S(2)}, u32[]{:S(2)}) async-start(f32[32,1,1664]{2,1,0:T(1,128)} %bitcast.1), calls=%async_computation | async-start | bytes 425984 | tf_op jit(solution)/shard_map/all_to_all | solution.py:569
  42.7 2.3 %copy-start = (bf16[10,2,256,512]{3,2,1,0:T(8,128)(2,1)}, bf16[10,2,256,512]{3,2,1,0:T(8,128)(2,1)S(1)}, u32[]{:S(2)}) copy-start(bf16[10,2,256,512]{3,2,1,0:T(8,128)(2,1)S(1)} %get-tuple-element.31.refs_4_) | copy-start | bytes 15728644
  73.5 3.5 %collective-permute-start = (f32[416,128]{1,0:T(8,128)S(1)}, f32[416,128]{1,0:T(8,128)S(1)}, u32[]{:S(2)}, u32[]{:S(2)}) collective-permute-start(f32[416,128]{1,0:T(8,128)S(1)} %bitcast.5), channel_id=1, source_target_pairs={{0,1},{1,0},{2,3},{3,2},{4,5},{5,4},{6,7},{7,6},{8,9},{9,8},{10,11... | collective-permute-start | bytes 638984 | tf_op jit(solution)/shard_map/ppermute | solution.py:577
  119.7 10.4 %collective-permute-start.1 = (f32[224,128]{1,0:T(8,128)S(1)}, f32[224,128]{1,0:T(8,128)S(1)}, u32[]{:S(2)}, u32[]{:S(2)}) collective-permute-start(f32[224,128]{1,0:T(8,128)S(1)} %bitcast.7), channel_id=1, source_target_pairs={{0,1},{1,0},{2,3},{3,2},{4,5},{5,4},{6,7},{7,6},{8,9},{9,8},{10,11... | collective-permute-start | bytes 344072 | tf_op jit(solution)/shard_map/ppermute | solution.py:581

commit v4 on v2

--- a/solution.py
+++ b/solution.py
@@ -163,7 +163,7 @@
     second = pair - norb * first
     inside = pair < norb * norb
     picks = [
-        jnp.where((2 * which + half == orb) & inside, 1.0, 0.0)
+        jnp.where((2 * which + half == orb) & inside, 1.0, 0.0).astype(jnp.bfloat16)
         for which in (first, second)
         for half in range(2)
     ]
@@ -172,7 +172,14 @@
     for i in range(norb):
         flat_ref[2 * i : 2 * i + 2, :bands] = proj_ref[0, i]
     flat = jnp.where(band_inside(flat_ref.shape, window_ref), flat_ref[...], 0.0)
-    picked = dot(flat, picks, (((0,), (0,)), ((), ())))
+    high = flat.astype(jnp.bfloat16)
+    middle, low = split(flat - high.astype(jnp.float32))
+    picked = lax.dot_general(
+        jnp.concatenate([high, middle, low], axis=0),
+        jnp.concatenate([picks, picks, picks], axis=0),
+        (((0,), (0,)), ((), ())),
+        preferred_element_type=jnp.float32,
+    )
     i_re, i_im, j_re, j_im = (picked[:, LANES * k : LANES * (k + 1)] for k in range(4))
     pair_re = (i_re * j_re + i_im * j_im)[:bands]
     pair_im = (i_im * j_re - i_re * j_im)[:bands]
@@ -193,33 +200,41 @@
         packed_ref[pl.ds(r, chips, stride=len(lines)), :] = line
 
 
+def own_sum(norb, chips, freqs, which, ref, wide_ref, mat_ref):
+    pairs = norb * norb
+    group = 2 * freqs
+    lines = spaced(ref, chips, norb, 2 * group)[group * which : group * (which + 1)]
+    mat = []
+    for half in range(2):
+        mat_ref[half] = upright(lines[freqs * half : freqs * (half + 1)])
+        mat.append([mat_ref[half, norb * i : norb * (i + 1), :] for i in range(norb)])
+    ainv = invert(*mat)
+    for half in range(2):
+        base = pairs * half
+        for i in range(norb):
+            at = base + norb * i
+            ainv[half][i] = ainv[half][i] - wide_ref[at : at + norb, :]
+    gorb_re, gorb_im = invert(*ainv)
+    return gorb_re + gorb_im
+
+
+def dress_kernel(norb, chips, freqs, own_ref, wide_ref, sum_ref, mat_ref):
+    for k, row in enumerate(own_sum(norb, chips, freqs, 0, own_ref, wide_ref, mat_ref)):
+        sum_ref[norb * k : norb * (k + 1), :] = row
+
+
 def dyson_kernel(
-    norb, chips, freqs, points, own_ref, sib_ref, wide_ref, new_ref, tile_ref,
-    mat_ref, turn_ref,
+    norb, chips, freqs, points, sib_ref, wide_ref, sum_ref, new_ref, tile_ref, mat_ref, turn_ref
 ):
     pairs = norb * norb
     group = 2 * freqs
-    lines = spaced(own_ref, chips, norb, 2 * group)[:group]
-    lines += spaced(sib_ref, chips, norb, 2 * group)[group:]
-    for half in range(2):
-        for part in range(2):
-            at = group * part + freqs * half
-            mat_ref[half, :, LANES * part : LANES * (part + 1)] = upright(lines[at : at + freqs])
+
     def rows(ref, base):
         return [ref[base + norb * i : base + norb * (i + 1), :] for i in range(norb)]
 
     sig_re, sig_im = rows(wide_ref, 0), rows(wide_ref, pairs)
-    for part in range(2):
-        lanes = pl.ds(LANES * part, LANES)
-        mat = [
-            [mat_ref[half, norb * i : norb * (i + 1), lanes] for i in range(norb)]
-            for half in range(2)
-        ]
-        ainv_re, ainv_im = invert(*mat)
-        gorb_re, gorb_im = invert(
-            [a - s for a, s in zip(ainv_re, sig_re)], [a - s for a, s in zip(ainv_im, sig_im)]
-        )
-        sums = [a + b for a, b in zip(sums, gorb_re + gorb_im)] if part else gorb_re + gorb_im
+    sums = own_sum(norb, chips, freqs, 1, sib_ref, wide_ref, mat_ref)
+    sums = [a + sum_ref[norb * k : norb * (k + 1), :] for k, a in enumerate(sums)]
     shift = chips // 2
     while shift:
         sums = [a + pltpu.roll(a, LANES - shift, 1) for a in sums]
@@ -237,10 +252,10 @@
         for i in range(norb):
             across = turn_ref[half, pl.ds(i, norb, stride=pitch), :]
             fresh = sig[i] + 0.5 * (diff[half][i] + sign * across)
-            mat_ref[half, norb * i : norb * (i + 1), :LANES] = fresh
+            mat_ref[half, norb * i : norb * (i + 1), :] = fresh
     lines = []
     for half in range(2):
-        flipped = mat_ref[half, :, :LANES].T
+        flipped = mat_ref[half].T
         lines += [flipped[chips * f : chips * f + 1] for f in range(freqs)]
     tile = jnp.concatenate(lines, axis=0)
     for half in range(2):
@@ -326,14 +341,10 @@
     denom = 1.0 / (energy * energy + freq * freq)
     green_re = -energy * denom
     green_im = -freq * denom
-    for j in range(norb):
-        p_re = flat[j : j + 1]
-        p_im = flat[STEP + j : STEP + j + 1]
-        re = split(green_re * p_re - green_im * p_im)
-        im = split(green_re * p_im + green_im * p_re)
-        for k in range(2):
-            right_ref[j, k, :, :span] = re[k]
-            right_ref[j, k, :, span:] = im[k]
+    re, im = split(green_re), split(green_im)
+    for k in range(2):
+        right_ref[k, :, :span] = re[k]
+        right_ref[k, :, span:] = im[k]
     side_ref[...] = jnp.zeros_like(side_ref)
     side_ref[:norb, :span] = flat[:norb]
     side_ref[:norb, span:] = flat[STEP : STEP + norb]
@@ -366,67 +377,61 @@
     return out
 
 
+def vertex_part(norb, chips, freqs, core_axis, which, ref, ainv_ref, vert_ref, end_ref, sig_ref):
+    core = lax.axis_index(core_axis)
+    group = 2 * freqs
+    lines = spaced(ref, chips, norb, group)
+    for half in range(2):
+        sig_ref[half] = upright(lines[freqs * half : freqs * (half + 1)])
+
+    def columns(ref, first):
+        return [ref[first, pl.ds(j, norb, stride=norb), :] for j in range(norb)]
+
+    sig = [columns(sig_ref, half) for half in range(2)]
+    mat = [
+        [a - s for a, s in zip(columns(ainv_ref, 2 * half + which), sig[half])] for half in range(2)
+    ]
+    turned = solve(mat, sig)
+    vert_ref[...] = jnp.zeros_like(vert_ref)
+    for j in range(norb):
+        sum_re, sum_im = sig[0][j], sig[1][j]
+        for k in range(norb):
+            y_re = turned[0][j][k : k + 1]
+            y_im = turned[1][j][k : k + 1]
+            sum_re = sum_re + (sig[0][k] * y_re - sig[1][k] * y_im)
+            sum_im = sum_im + (sig[0][k] * y_im + sig[1][k] * y_re)
+        at = 2 * LANES * j
+        vert_ref[0:norb, at : at + LANES] = sum_re
+        vert_ref[STEP : STEP + norb, at : at + LANES] = sum_im
+        at += LANES
+        vert_ref[0:norb, at : at + LANES] = sum_im
+        vert_ref[STEP : STEP + norb, at : at + LANES] = -sum_re
+    number = numbers((norb, 2 * LANES), chips, freqs, core)[:, LANES * which : LANES * (which + 1)]
+    last = number == 2 * freqs * chips - 1
+    orb = iota((norb, LANES), 1)
+    end_ref[...] = jnp.zeros_like(end_ref)
+    for half in range(2):
+        end = jnp.zeros((norb, LANES), jnp.float32)
+        for j in range(norb):
+            entry = jnp.where(last, sig[half][j], 0.0)
+            end = jnp.where(orb == j, jnp.sum(entry, axis=1, keepdims=True), end)
+        end_ref[STEP * half : STEP * half + norb, :LANES] = end
+        at = STEP * (1 - half)
+        end_ref[at : at + norb, LANES:] = -end if half == 0 else end
+
+
+def vertex_kernel(norb, chips, freqs, core_axis, own_ref, ainv_ref, vert_ref, end_ref, sig_ref):
+    vertex_part(norb, chips, freqs, core_axis, 0, own_ref, ainv_ref, vert_ref, end_ref, sig_ref)
+
+
 def density_kernel(
-    norb, chips, freqs, core_axis, ainv_ref, green_ref, left_ref, side_ref, right_ref, own_ref, sib_ref,
-    out_ref, sig_ref, vert_ref, sums_ref, held_ref, done,
+    norb, chips, freqs, core_axis, ainv_ref, green_ref, left_ref, side_ref, right_ref,
+    first_ref, start_ref, sib_ref, out_ref, sig_ref, vert_ref, end_ref, sums_ref,
 ):
-    core = lax.axis_index(core_axis)
-    fetches = [
-        pltpu.make_async_copy(right_ref.at[j], held_ref.at[j], done.at[j]) for j in range(norb)
-    ]
-    for fetch in fetches:
-        fetch.start()
-    group = 2 * freqs
     bands = out_ref.shape[2]
     tall = green_ref.shape[1]
     count = green_ref.shape[2]
-    wide = 2 * STEP
-    for part in range(2):
-        lines = spaced((own_ref, sib_ref)[part], chips, norb, group)
-        for half in range(2):
-            sig_ref[2 * half + part] = upright(lines[freqs * half : freqs * (half + 1)])
-
-    def columns(ref, half, part):
-        return [ref[2 * half + part, pl.ds(j, norb, stride=norb), :] for j in range(norb)]
-
-    spare = jnp.zeros((STEP - norb, 2 * norb * count), jnp.float32)
-    vert_ref[norb:STEP] = spare
-    vert_ref[STEP + norb : wide] = spare
-    for part in range(2):
-        sig = [columns(sig_ref, half, part) for half in range(2)]
-        mat = [
-            [a - s for a, s in zip(columns(ainv_ref, half, part), sig[half])] for half in range(2)
-        ]
-        turned = solve(mat, sig)
-        for j in range(norb):
-            sum_re, sum_im = sig[0][j], sig[1][j]
-            for k in range(norb):
-                y_re = turned[0][j][k : k + 1]
-                y_im = turned[1][j][k : k + 1]
-                sum_re = sum_re + (sig[0][k] * y_re - sig[1][k] * y_im)
-                sum_im = sum_im + (sig[0][k] * y_im + sig[1][k] * y_re)
-            at = 2 * count * j + LANES * part
-            vert_ref[0:norb, at : at + LANES] = sum_re
-            vert_ref[STEP : STEP + norb, at : at + LANES] = sum_im
-            at += count
-            vert_ref[0:norb, at : at + LANES] = sum_im
-            vert_ref[STEP : STEP + norb, at : at + LANES] = -sum_re
-
-    last = numbers((norb, count), chips, freqs, core) == count - 1
-    orb = iota((norb, LANES), 1)
-    ends = []
-    for half in range(2):
-        end = jnp.zeros((norb, LANES), jnp.float32)
-        for j in range(norb):
-            for part in range(2):
-                spot = last[:, LANES * part : LANES * (part + 1)]
-                entry = jnp.where(spot, columns(sig_ref, half, part)[j], 0.0)
-                end = end + jnp.where(orb == j, jnp.sum(entry, axis=1, keepdims=True), 0.0)
-        ends.append(end)
-    blank = jnp.zeros((STEP - norb, LANES), jnp.float32)
-    ends = [
-        jnp.concatenate([a, blank, b, blank], axis=0) for a, b in (ends, (ends[1], -ends[0]))
-    ]
+    vertex_part(norb, chips, freqs, core_axis, 1, sib_ref, ainv_ref, vert_ref, end_ref, sig_ref)
     left = left_ref[...]
 
     def mixed(block):
@@ -434,27 +439,40 @@
         stacked = jnp.concatenate([high, low, high], axis=0)
         return lax.dot_general(left, stacked, NN, preferred_element_type=jnp.float32)
 
+    def doubled(halves):
+        size = halves[0].shape[1] // 2
+        turned = [jnp.concatenate([-h[:, size:], h[:, :size]], axis=1) for h in halves]
+        return [jnp.concatenate([a, b], axis=0) for a, b in zip(halves, turned)]
+
     def join(re, im, right):
-        size = right[0].shape[1] // 2
         left = [jnp.concatenate([r, i], axis=1) for r, i in zip(split(re), split(im))]
-        turned = [jnp.concatenate([-h[:, size:], h[:, :size]], axis=1) for h in right]
-        return dot3(left, [jnp.concatenate([a, b], axis=0) for a, b in zip(right, turned)], NN)
+        return dot3(left, right, NN)
 
     weight = -0.5 * inverse_temp * tail_weight(count)
-    tail = weight * mixed(jnp.concatenate(ends, axis=1))
-    total = join(tail[:, :LANES], tail[:, LANES:], split(side_ref[...]))
+    tail = weight * mixed(start_ref[...] + end_ref[...])
+    total = join(tail[:, :LANES], tail[:, LANES:], doubled(split(side_ref[...])))
+    span = sums_ref.shape[1]
+    total_re, total_im = total[:, :span], total[:, span:]
+    right = doubled([right_ref[k] for k in range(2)])
     green_re, green_im = green_ref[0], green_ref[1]
     for j in range(norb):
-        mix = mixed(vert_ref[:, 2 * count * j : 2 * count * (j + 1)])
+        block = []
+        for half in range(2):
+            at = LANES * (2 * j + half)
+            block += [first_ref[:, at : at + LANES], vert_ref[:, at : at + LANES]]
+        mix = mixed(jnp.concatenate(block, axis=1))
         mix_re, mix_im = mix[:, :count], mix[:, count:]
         side_re = mix_re * green_re - mix_im * green_im
         side_im = mix_re * green_im + mix_im * green_re
-        fetches[j].wait()
-        total = total + join(side_re, side_im, [held_ref[j, k] for k in range(2)])
-    span = sums_ref.shape[1]
+        both = join(side_re, side_im, right)
+        both_re, both_im = both[:, :span], both[:, span:]
+        p_re = side_ref[j : j + 1, :span]
+        p_im = side_ref[j : j + 1, span:]
+        total_re = total_re + (both_re * p_re - both_im * p_im)
+        total_im = total_im + (both_re * p_im + both_im * p_re)
     sums_ref[...] = jnp.zeros_like(sums_ref)
-    for half, sign in ((0, 1.0), (1, -1.0)):
-        sums_ref[:tall, :] = total[:, span * half : span * (half + 1)]
+    for half, total, sign in ((0, total_re, 1.0), (1, total_im, -1.0)):
+        sums_ref[:tall, :] = total
         both = sums_ref[...] + sign * sums_ref[...].T
         out_ref[0, half] = both[:bands, :bands] / inverse_temp
 
@@ -501,6 +519,12 @@
     def prepare(*refs):
         prepare_kernel(norb, chips, freqs, axis, *refs)
 
+    def dress(*refs):
+        dress_kernel(norb, chips, freqs, *refs)
+
+    def vertex(*refs):
+        vertex_kernel(norb, chips, freqs, axis, *refs)
+
     def rebuild(*refs):
         density_kernel(norb, chips, freqs, axis, *refs)
 
@@ -513,13 +537,20 @@
         project,
         (struct(chips * long, LANES), struct(2 * count, LANES)),
         [HBM] * 3,
-        [*inputs, scratch(24, wide), pltpu.SemaphoreType.DMA((3,))],
+        [*inputs, scratch(32, wide), pltpu.SemaphoreType.DMA((3,))],
     )
     second = run(
         dyson,
         (struct(2, norb, freqs, norb), struct(chips * short, LANES)),
         [VMEM] * 3,
-        [scratch(2, LANES, 2 * LANES), scratch(2, 16 * norb, LANES)],
+        [scratch(2, LANES, LANES), scratch(2, 16 * norb, LANES)],
+    )
+    before = run(dress, struct(2 * pairs, LANES), [VMEM] * 2, [scratch(2, LANES, LANES)])
+    after = run(
+        vertex,
+        (struct(2 * STEP, 2 * norb * LANES), struct(2 * STEP, 2 * LANES)),
+        [VMEM] * 2,
+        [scratch(2, LANES, LANES)],
     )
     aside = run(
         prepare,
@@ -528,7 +559,7 @@
             struct(2, tall, count),
             struct(tall, 6 * STEP, dtype=jnp.bfloat16),
             struct(LANES, 2 * wide),
-            struct(norb, 2, count, 2 * wide, dtype=jnp.bfloat16),
+            struct(2, count, 2 * wide, dtype=jnp.bfloat16),
             struct(4 * pairs, LANES),
         ),
         [HBM] * 3 + [VMEM] * 3,
@@ -542,16 +573,15 @@
     third = run(
         rebuild,
         struct(1, 2, bands, bands),
-        [VMEM] * 4 + [HBM] + [VMEM] * 2,
+        [VMEM] * 8,
         [
-            scratch(4, LANES, LANES),
-            scratch(2 * STEP, 2 * norb * count),
+            scratch(2, LANES, LANES),
+            scratch(2 * STEP, 2 * norb * LANES),
+            scratch(2 * STEP, 2 * LANES),
             scratch(wide, wide),
-            pltpu.VMEM((norb, 2, count, 2 * wide), jnp.bfloat16),
-            pltpu.SemaphoreType.DMA((norb,)),
         ],
     )
-    return first, aside, second, third
+    return first, aside, before, second, after, third
 
 
 def local(energies, proj, window, sigma, impurity_inverse):
@@ -560,7 +590,7 @@
     chips = lax.axis_size("z")
     cores = lax.axis_size("core")
     points = energies.shape[0] * chips * cores
-    first, aside, second, third = kernels(norb, bands, freqs, chips, cores, points)
+    first, aside, before, second, after, third = kernels(norb, bands, freqs, chips, cores, points)
     swap = [(0, 1), (1, 0)]
     proj = jnp.swapaxes(proj, 1, 2)
 
@@ -573,10 +603,11 @@
     ready = aside(*far, sigma, impurity_inverse, plain)
     got, ready = lax.optimization_barrier((across(packed), ready))
     *ready, spread = ready
-    sigma_new, tiles = second(got, lax.ppermute(got, "core", swap), spread)
+    sibling = lax.ppermute(got, "core", swap)
+    sigma_new, tiles = second(sibling, spread, before(got, spread))
     back = across(tiles)
-    ready[4] = pltpu.with_memory_space_constraint(ready[4], pltpu.HBM)
-    density = third(*ready, back, lax.ppermute(back, "core", swap))
+    sibling = lax.ppermute(back, "core", swap)
+    density = third(*ready, *after(back, ready[0]), sibling)
     return density, jnp.swapaxes(sigma_new, 2, 3)
 
 

time: 124 us -> 121 us (0.976)
  Pallas kernels: 18.2 us -> 14.5 us
  waiting for transfers between devices: 30.7 us -> 34.2 us
  local copies, waits for them, and re-layouts: 4.32 us -> 1.01 us
    all_to_all x1, waiting for transfers between devices: 28.6 us -> 33.8 us  [across(): got = lax.all_to_all(rows.reshape(chips, 1, -1), 'z', 0, 0, tiled=True)]
    unnamed x4 -> x6, local copies, waits for them, and re-layouts: 4.32 us -> 1.01 us
    pallas_call x1, Pallas kernels: 3.24 us -> 1.36 us  [local(): ready = aside(*far, sigma, impurity_inverse, plain)]
    ppermute x2, waiting for transfers between devices: 2.06 us -> 0.38 us  [the longest x1 0.38 us: local(): sibling = lax.ppermute(got, 'core', swap)]
    pallas_call x2 -> x4, Pallas kernels: 11.4 us -> 10.6 us  [the longest x2 7.7 us: local(): density = third(*ready, *after(back, ready[0]), sibling)]
  transfers between devices with their start and end apart: 3 -> 3, of which waited for: 3 -> 2; matrix products, arithmetic and copies ran while one was open for 2% -> 0% of each run, Pallas kernels for 3% -> 3%
where the time goes in v4:
time: 121 us; the launch traced here: 120 us
  starting transfers between devices  37.6 us (31%)
  waiting for transfers between devices  34.2 us (28%)
  blocking collectives  32.1 us (27%)
  Pallas kernels  14.5 us (12%)
    all_to_all x1, waiting for transfers between devices, across(): got = lax.all_to_all(rows.reshape(chips, 1, -1), 'z', 0, 0, tiled=True)  33.8 us
    all_to_all x1, starting transfers between devices, across(): got = lax.all_to_all(rows.reshape(chips, 1, -1), 'z', 0, 0, tiled=True)  33.2 us
    all_to_all x1, blocking collectives, across(): got = lax.all_to_all(rows.reshape(chips, 1, -1), 'z', 0, 0, tiled=True)  32.1 us
    pallas_call x2, Pallas kernels, local(): density = third(*ready, *after(back, ready[0]), sibling)  7.7 us
    pallas_call x2, Pallas kernels, local(): sigma_new, tiles = second(sibling, spread, before(got, spread))  2.92 us
    pallas_call x1, Pallas kernels, local(): packed, plain = first(*far)  2.48 us
  transfers between devices with their start and end apart: 3, of which 2 were waited for; matrix products, arithmetic and copies ran while one was open for 0% of the time, Pallas kernels for 3%

profile of v4, /device:TPU:37, one launch (start us, length us, event | category | flops | bytes accessed | tf_op | source)
XLA Modules:
  0.0 120.1 jit_solution(16182203809377528342)
XLA Ops:
  0.6 2.5 %shard_map.68 = (f32[416,128]{1,0:T(8,128)}, f32[512,128]{1,0:T(8,128)S(1)}) custom-call(f32[1,200]{1,0:T(1,128)} %refs_0_.3, f32[1,10,2,200]{3,2,1,0:T(2,128)} %bitcast.11, s32[1,2]{1,0:T(1,128)} %refs_2_.3), custom_call_target="tpu_custom_call" | custom-call | tf_op jit(solution)/shard_map/pallas_call | solution.py:602
  3.1 0.0 copy-start
  3.1 33.2 %all-to-all-start = ((f32[32,1,1664]{2,1,0:T(1,128)}), f32[32,1,1664]{2,1,0:T(1,128)S(1)}, u32[]{:S(2)}, u32[]{:S(2)}) async-start(f32[32,1,1664]{2,1,0:T(1,128)} %bitcast.1), calls=%async_computation | async-start | bytes 425984 | tf_op jit(solution)/shard_map/all_to_all | solution.py:598
  36.3 0.0 copy-done
  36.4 0.0 copy-start.1
  36.4 0.2 copy.10.refs_3_
  36.6 0.5 copy-done.1
  37.1 0.2 copy.11.refs_4_
  37.4 1.4 %shard_map.69 = (f32[4,100,128]{2,1,0:T(8,128)S(1)}, f32[2,208,256]{2,1,0:T(8,128)S(1)}, bf16[208,96]{1,0:T(8,128)(2,1)S(1)}, f32[128,512]{1,0:T(8,128)S(1)}, bf...) custom-call(f32[1,200]{1,0:T(1,128)} %refs_0_.3, f32[1,10,2,200]{3,2,1,0:T(2,128)} %bitcast.12, s32[1,2]{1,0:T(1,128)} %refs_2_.3, ...), custom_call_target="tpu_custom_call" | custom-call | tf_op jit(solution)/shard_map/pallas_call | solution.py:603
  38.7 33.8 %all-to-all-done = f32[32,1,1664]{2,1,0:T(1,128)S(1)} async-done(((f32[32,1,1664]{2,1,0:T(1,128)}), f32[32,1,1664]{2,1,0:T(1,128)S(1)}, u32[]{:S(2)}, u32[]{:S(2)}) %all-to-all-start) | async-done | bytes 213024 | tf_op jit(solution)/shard_map/all_to_all | solution.py:598
  72.6 2.4 %collective-permute-start = (f32[416,128]{1,0:T(8,128)S(1)}, f32[416,128]{1,0:T(8,128)S(1)}, u32[]{:S(2)}, u32[]{:S(2)}) collective-permute-start(f32[416,128]{1,0:T(8,128)S(1)} %bitcast.6), channel_id=1, source_target_pairs={{0,1},{1,0},{2,3},{3,2},{4,5},{5,4},{6,7},{7,6},{8,9},{9,8},{10,11... | collective-permute-start | bytes 638984 | tf_op jit(solution)/shard_map/ppermute | solution.py:606
  75.0 0.7 shard_map.70.refs_2_
  75.7 0.4 collective-permute-done.refs_0_
  76.1 2.2 %shard_map.71 = (f32[2,10,4,10]{3,2,1,0:T(4,128)}, f32[224,128]{1,0:T(8,128)S(1)}) custom-call(f32[416,128]{1,0:T(8,128)S(1)} %collective-permute-done.refs_0_, f32[400,128]{1,0:T(8,128)S(1)} %get-tuple-element.35.refs_1_, f32[200,128]{1,0:T(8,128)S(1)} %shard_map.70.refs_2_), custom_call_target="tpu_custom_call" | custom-call | tf_op jit(solution)/shard_map/pallas_call | solution.py:607
  78.3 32.1 %all_to_all.10 = f32[32,1,896]{2,1,0:T(1,128)S(1)} all-to-all(f32[32,1,896]{2,1,0:T(1,128)S(1)} %bitcast.10), channel_id=1, replica_groups=mesh['parts'=4,'z'=32,'core'=2] {'z'}, dimensions={0} | all-to-all | bytes 229376 | tf_op jit(solution)/shard_map/all_to_all | solution.py:598
  110.4 2.0 %collective-permute-start.1 = (f32[224,128]{1,0:T(8,128)S(1)}, f32[224,128]{1,0:T(8,128)S(1)}, u32[]{:S(2)}, u32[]{:S(2)}) collective-permute-start(f32[224,128]{1,0:T(8,128)S(1)} %bitcast.8), channel_id=1, source_target_pairs={{0,1},{1,0},{2,3},{3,2},{4,5},{5,4},{6,7},{7,6},{8,9},{9,8},{10,11... | collective-permute-start | bytes 344072 | tf_op jit(solution)/shard_map/ppermute | solution.py:609
  112.4 1.0 shard_map.72
  113.4 0.0 collective-permute-done.1.refs_7_
  113.4 6.7 %shard_map.73 = f32[1,2,200,200]{3,2,1,0:T(8,128)} custom-call(f32[4,100,128]{2,1,0:T(8,128)S(1)} %get-tuple-element.29.refs_1_.refs_0_, f32[2,208,256]{2,1,0:T(8,128)S(1)} %get-tuple-element.30.refs_1_, bf16[208,96]{1,0:T(8,128)(2,1)S(1)} %get-tuple-element.31.refs_2_, f32[128,512]{1,0:T(8,128)S(1)} %get-tuple-element.32.refs_3_, ...), custom_call_target="tpu_custom_call" | custom-call | tf_op jit(solution)/shard_map/pallas_call | solution.py:610
Async XLA Ops:
  3.1 33.2 %copy-start = (f32[2,10,10,4]{2,3,1,0:T(4,128)S(1)}, f32[2,10,10,4]{2,3,1,0:T(4,128)}, u32[]{:S(2)}) copy-start(f32[2,10,10,4]{2,3,1,0:T(4,128)} %param.8) | copy-start | bytes 9604
  3.1 69.4 %all-to-all-start = ((f32[32,1,1664]{2,1,0:T(1,128)}), f32[32,1,1664]{2,1,0:T(1,128)S(1)}, u32[]{:S(2)}, u32[]{:S(2)}) async-start(f32[32,1,1664]{2,1,0:T(1,128)} %bitcast.1), calls=%async_computation | async-start | bytes 425984 | tf_op jit(solution)/shard_map/all_to_all | solution.py:598
  36.4 0.8 copy-start.1
  72.6 3.5 %collective-permute-start = (f32[416,128]{1,0:T(8,128)S(1)}, f32[416,128]{1,0:T(8,128)S(1)}, u32[]{:S(2)}, u32[]{:S(2)}) collective-permute-start(f32[416,128]{1,0:T(8,128)S(1)} %bitcast.6), channel_id=1, source_target_pairs={{0,1},{1,0},{2,3},{3,2},{4,5},{5,4},{6,7},{7,6},{8,9},{9,8},{10,11... | collective-permute-start | bytes 638984 | tf_op jit(solution)/shard_map/ppermute | solution.py:606
  110.4 3.0 %collective-permute-start.1 = (f32[224,128]{1,0:T(8,128)S(1)}, f32[224,128]{1,0:T(8,128)S(1)}, u32[]{:S(2)}, u32[]{:S(2)}) collective-permute-start(f32[224,128]{1,0:T(8,128)S(1)} %bitcast.8), channel_id=1, source_target_pairs={{0,1},{1,0},{2,3},{3,2},{4,5},{5,4},{6,7},{7,6},{8,9},{9,8},{10,11... | collective-permute-start | bytes 344072 | tf_op jit(solution)/shard_map/ppermute | solution.py:609

commit v5 on v4

--- a/solution.py
+++ b/solution.py
@@ -453,7 +453,12 @@
     total = join(tail[:, :LANES], tail[:, LANES:], doubled(split(side_ref[...])))
     span = sums_ref.shape[1]
     total_re, total_im = total[:, :span], total[:, span:]
-    right = doubled([right_ref[k] for k in range(2)])
+    right_re = [right_ref[k, :, :span] for k in range(2)]
+    right_im = [right_ref[k, :, span:] for k in range(2)]
+    right_sum = split(
+        (right_re[0].astype(jnp.float32) + right_im[0].astype(jnp.float32))
+        + (right_re[1].astype(jnp.float32) + right_im[1].astype(jnp.float32))
+    )
     green_re, green_im = green_ref[0], green_ref[1]
     for j in range(norb):
         block = []
@@ -464,8 +469,11 @@
         mix_re, mix_im = mix[:, :count], mix[:, count:]
         side_re = mix_re * green_re - mix_im * green_im
         side_im = mix_re * green_im + mix_im * green_re
-        both = join(side_re, side_im, right)
-        both_re, both_im = both[:, :span], both[:, span:]
+        prod_re = dot3(split(side_re), right_re, NN)
+        prod_im = dot3(split(side_im), right_im, NN)
+        prod_sum = dot3(split(side_re + side_im), right_sum, NN)
+        both_re = prod_re - prod_im
+        both_im = prod_sum - prod_re - prod_im
         p_re = side_ref[j : j + 1, :span]
         p_im = side_ref[j : j + 1, span:]
         total_re = total_re + (both_re * p_re - both_im * p_im)

time: 121 us -> 120 us (level)
  no operation moved by 1% of the time
where the time goes in v5:
time: 120 us
  starting transfers between devices  37.6 us (31%)
  waiting for transfers between devices  34.2 us (29%)
  blocking collectives  32.1 us (27%)
  Pallas kernels  14 us (12%)
    all_to_all x1, waiting for transfers between devices, across(): got = lax.all_to_all(rows.reshape(chips, 1, -1), 'z', 0, 0, tiled=True)  33.8 us
    all_to_all x1, starting transfers between devices, across(): got = lax.all_to_all(rows.reshape(chips, 1, -1), 'z', 0, 0, tiled=True)  33.2 us
    all_to_all x1, blocking collectives, across(): got = lax.all_to_all(rows.reshape(chips, 1, -1), 'z', 0, 0, tiled=True)  32.1 us
    pallas_call x2, Pallas kernels, local(): density = third(*ready, *after(back, ready[0]), sibling)  7.29 us
    pallas_call x2, Pallas kernels, local(): sigma_new, tiles = second(sibling, spread, before(got, spread))  2.92 us
    pallas_call x1, Pallas kernels, local(): packed, plain = first(*far)  2.48 us
    ppermute x1, starting transfers between devices, local(): sibling = lax.ppermute(got, 'core', swap)  2.41 us
  transfers between devices with their start and end apart: 3, of which 2 were waited for; matrix products, arithmetic and copies ran while one was open for 0% of the time, Pallas kernels for 3%

profile of v5, /device:TPU:37, one launch (start us, length us, event | category | flops | bytes accessed | tf_op | source)
XLA Modules:
  0.0 119.7 jit_solution(16836599315642315445)
XLA Ops:
  0.6 2.5 %shard_map.68 = (f32[416,128]{1,0:T(8,128)}, f32[512,128]{1,0:T(8,128)S(1)}) custom-call(f32[1,200]{1,0:T(1,128)} %refs_0_.3, f32[1,10,2,200]{3,2,1,0:T(2,128)} %bitcast.11, s32[1,2]{1,0:T(1,128)} %refs_2_.3), custom_call_target="tpu_custom_call" | custom-call | tf_op jit(solution)/shard_map/pallas_call | solution.py:610
  3.1 0.0 copy-start
  3.1 33.2 %all-to-all-start = ((f32[32,1,1664]{2,1,0:T(1,128)}), f32[32,1,1664]{2,1,0:T(1,128)S(1)}, u32[]{:S(2)}, u32[]{:S(2)}) async-start(f32[32,1,1664]{2,1,0:T(1,128)} %bitcast.1), calls=%async_computation | async-start | bytes 425984 | tf_op jit(solution)/shard_map/all_to_all | solution.py:606
  36.3 0.0 copy-done
  36.4 0.0 copy-start.1
  36.4 0.2 copy.10.refs_3_
  36.6 0.5 copy-done.1
  37.1 0.2 copy.11.refs_4_
  37.4 1.4 %shard_map.69 = (f32[4,100,128]{2,1,0:T(8,128)S(1)}, f32[2,208,256]{2,1,0:T(8,128)S(1)}, bf16[208,96]{1,0:T(8,128)(2,1)S(1)}, f32[128,512]{1,0:T(8,128)S(1)}, bf...) custom-call(f32[1,200]{1,0:T(1,128)} %refs_0_.3, f32[1,10,2,200]{3,2,1,0:T(2,128)} %bitcast.12, s32[1,2]{1,0:T(1,128)} %refs_2_.3, ...), custom_call_target="tpu_custom_call" | custom-call | tf_op jit(solution)/shard_map/pallas_call | solution.py:611
  38.7 33.8 %all-to-all-done = f32[32,1,1664]{2,1,0:T(1,128)S(1)} async-done(((f32[32,1,1664]{2,1,0:T(1,128)}), f32[32,1,1664]{2,1,0:T(1,128)S(1)}, u32[]{:S(2)}, u32[]{:S(2)}) %all-to-all-start) | async-done | bytes 213024 | tf_op jit(solution)/shard_map/all_to_all | solution.py:606
  72.6 2.4 %collective-permute-start = (f32[416,128]{1,0:T(8,128)S(1)}, f32[416,128]{1,0:T(8,128)S(1)}, u32[]{:S(2)}, u32[]{:S(2)}) collective-permute-start(f32[416,128]{1,0:T(8,128)S(1)} %bitcast.6), channel_id=1, source_target_pairs={{0,1},{1,0},{2,3},{3,2},{4,5},{5,4},{6,7},{7,6},{8,9},{9,8},{10,11... | collective-permute-start | bytes 638984 | tf_op jit(solution)/shard_map/ppermute | solution.py:614
  75.0 0.7 shard_map.70.refs_2_
  75.7 0.4 collective-permute-done.refs_0_
  76.1 2.2 %shard_map.71 = (f32[2,10,4,10]{3,2,1,0:T(4,128)}, f32[224,128]{1,0:T(8,128)S(1)}) custom-call(f32[416,128]{1,0:T(8,128)S(1)} %collective-permute-done.refs_0_, f32[400,128]{1,0:T(8,128)S(1)} %get-tuple-element.35.refs_1_, f32[200,128]{1,0:T(8,128)S(1)} %shard_map.70.refs_2_), custom_call_target="tpu_custom_call" | custom-call | tf_op jit(solution)/shard_map/pallas_call | solution.py:615
  78.3 32.1 %all_to_all.10 = f32[32,1,896]{2,1,0:T(1,128)S(1)} all-to-all(f32[32,1,896]{2,1,0:T(1,128)S(1)} %bitcast.10), channel_id=1, replica_groups=mesh['parts'=4,'z'=32,'core'=2] {'z'}, dimensions={0} | all-to-all | bytes 229376 | tf_op jit(solution)/shard_map/all_to_all | solution.py:606
  110.4 2.0 %collective-permute-start.1 = (f32[224,128]{1,0:T(8,128)S(1)}, f32[224,128]{1,0:T(8,128)S(1)}, u32[]{:S(2)}, u32[]{:S(2)}) collective-permute-start(f32[224,128]{1,0:T(8,128)S(1)} %bitcast.8), channel_id=1, source_target_pairs={{0,1},{1,0},{2,3},{3,2},{4,5},{5,4},{6,7},{7,6},{8,9},{9,8},{10,11... | collective-permute-start | bytes 344072 | tf_op jit(solution)/shard_map/ppermute | solution.py:617
  112.4 1.0 shard_map.72
  113.4 0.0 collective-permute-done.1.refs_7_
  113.4 6.3 %shard_map.73 = f32[1,2,200,200]{3,2,1,0:T(8,128)} custom-call(f32[4,100,128]{2,1,0:T(8,128)S(1)} %get-tuple-element.29.refs_1_.refs_0_, f32[2,208,256]{2,1,0:T(8,128)S(1)} %get-tuple-element.30.refs_1_, bf16[208,96]{1,0:T(8,128)(2,1)S(1)} %get-tuple-element.31.refs_2_, f32[128,512]{1,0:T(8,128)S(1)} %get-tuple-element.32.refs_3_, ...), custom_call_target="tpu_custom_call" | custom-call | tf_op jit(solution)/shard_map/pallas_call | solution.py:618
Async XLA Ops:
  3.1 33.2 %copy-start = (f32[2,10,10,4]{2,3,1,0:T(4,128)S(1)}, f32[2,10,10,4]{2,3,1,0:T(4,128)}, u32[]{:S(2)}) copy-start(f32[2,10,10,4]{2,3,1,0:T(4,128)} %param.8) | copy-start | bytes 9604
  3.1 69.4 %all-to-all-start = ((f32[32,1,1664]{2,1,0:T(1,128)}), f32[32,1,1664]{2,1,0:T(1,128)S(1)}, u32[]{:S(2)}, u32[]{:S(2)}) async-start(f32[32,1,1664]{2,1,0:T(1,128)} %bitcast.1), calls=%async_computation | async-start | bytes 425984 | tf_op jit(solution)/shard_map/all_to_all | solution.py:606
  36.4 0.8 copy-start.1
  72.6 3.5 %collective-permute-start = (f32[416,128]{1,0:T(8,128)S(1)}, f32[416,128]{1,0:T(8,128)S(1)}, u32[]{:S(2)}, u32[]{:S(2)}) collective-permute-start(f32[416,128]{1,0:T(8,128)S(1)} %bitcast.6), channel_id=1, source_target_pairs={{0,1},{1,0},{2,3},{3,2},{4,5},{5,4},{6,7},{7,6},{8,9},{9,8},{10,11... | collective-permute-start | bytes 638984 | tf_op jit(solution)/shard_map/ppermute | solution.py:614
  110.4 3.0 %collective-permute-start.1 = (f32[224,128]{1,0:T(8,128)S(1)}, f32[224,128]{1,0:T(8,128)S(1)}, u32[]{:S(2)}, u32[]{:S(2)}) collective-permute-start(f32[224,128]{1,0:T(8,128)S(1)} %bitcast.8), channel_id=1, source_target_pairs={{0,1},{1,0},{2,3},{3,2},{4,5},{5,4},{6,7},{7,6},{8,9},{9,8},{10,11... | collective-permute-start | bytes 344072 | tf_op jit(solution)/shard_map/ppermute | solution.py:617

commit v6 on v5

--- a/solution.py
+++ b/solution.py
@@ -224,7 +224,7 @@
 
 
 def dyson_kernel(
-    norb, chips, freqs, points, sib_ref, wide_ref, sum_ref, new_ref, tile_ref, mat_ref, turn_ref
+    norb, chips, freqs, points, sib_ref, wide_ref, sum_ref, tile_ref, mat_ref, turn_ref
 ):
     pairs = norb * norb
     group = 2 * freqs
@@ -257,10 +257,6 @@
     for half in range(2):
         flipped = mat_ref[half].T
         lines += [flipped[chips * f : chips * f + 1] for f in range(freqs)]
-    tile = jnp.concatenate(lines, axis=0)
-    for half in range(2):
-        for i in range(norb):
-            new_ref[half, i] = tile[freqs * half : freqs * (half + 1), norb * i : norb * (i + 1)]
     lines = pack(lines, norb)
     for r, line in enumerate(lines):
         tile_ref[pl.ds(r, chips, stride=len(lines)), :] = jnp.broadcast_to(line, (chips, LANES))
@@ -426,8 +422,14 @@
 
 def density_kernel(
     norb, chips, freqs, core_axis, ainv_ref, green_ref, left_ref, side_ref, right_ref,
-    first_ref, start_ref, sib_ref, out_ref, sig_ref, vert_ref, end_ref, sums_ref,
+    first_ref, start_ref, tile_ref, sib_ref, out_ref, new_ref, sig_ref, vert_ref, end_ref, sums_ref,
 ):
+    group = 2 * freqs
+    kept = kept_rows(norb, group)
+    tile = jnp.concatenate(unpack([tile_ref[k : k + 1, :] for k in range(kept)], norb, group), axis=0)
+    for half in range(2):
+        for i in range(norb):
+            new_ref[half, i] = tile[freqs * half : freqs * (half + 1), norb * i : norb * (i + 1)]
     bands = out_ref.shape[2]
     tall = green_ref.shape[1]
     count = green_ref.shape[2]
@@ -549,7 +551,7 @@
     )
     second = run(
         dyson,
-        (struct(2, norb, freqs, norb), struct(chips * short, LANES)),
+        struct(chips * short, LANES),
         [VMEM] * 3,
         [scratch(2, LANES, LANES), scratch(2, 16 * norb, LANES)],
     )
@@ -580,8 +582,8 @@
     )
     third = run(
         rebuild,
-        struct(1, 2, bands, bands),
-        [VMEM] * 8,
+        (struct(1, 2, bands, bands), struct(2, norb, freqs, norb)),
+        [VMEM] * 9,
         [
             scratch(2, LANES, LANES),
             scratch(2 * STEP, 2 * norb * LANES),
@@ -612,10 +614,10 @@
     got, ready = lax.optimization_barrier((across(packed), ready))
     *ready, spread = ready
     sibling = lax.ppermute(got, "core", swap)
-    sigma_new, tiles = second(sibling, spread, before(got, spread))
+    tiles = second(sibling, spread, before(got, spread))
     back = across(tiles)
     sibling = lax.ppermute(back, "core", swap)
-    density = third(*ready, *after(back, ready[0]), sibling)
+    density, sigma_new = third(*ready, *after(back, ready[0]), tiles, sibling)
     return density, jnp.swapaxes(sigma_new, 2, 3)
 
 

time: 120 us -> 120 us (level)
  no operation moved by 1% of the time
where the time goes in v6:
time: 120 us; the launch traced here: 119 us
  starting transfers between devices  37.6 us (31%)
  waiting for transfers between devices  34.2 us (29%)
  blocking collectives  32.2 us (27%)
  Pallas kernels  13.4 us (11%)
    all_to_all x1, waiting for transfers between devices, across(): got = lax.all_to_all(rows.reshape(chips, 1, -1), 'z', 0, 0, tiled=True)  33.8 us
    all_to_all x1, starting transfers between devices, across(): got = lax.all_to_all(rows.reshape(chips, 1, -1), 'z', 0, 0, tiled=True)  33.2 us
    all_to_all x1, blocking collectives, across(): got = lax.all_to_all(rows.reshape(chips, 1, -1), 'z', 0, 0, tiled=True)  32.2 us
    pallas_call x2, Pallas kernels, local(): density, sigma_new = third(*ready, *after(back, ready[0]), tiles, sibling)  7.28 us
    pallas_call x1, Pallas kernels, local(): packed, plain = first(*far)  2.48 us
    ppermute x1, starting transfers between devices, local(): sibling = lax.ppermute(got, 'core', swap)  2.41 us
  transfers between devices with their start and end apart: 3, of which 2 were waited for; matrix products, arithmetic and copies ran while one was open for 0% of the time, Pallas kernels for 3%

profile of v6, /device:TPU:37, one launch (start us, length us, event | category | flops | bytes accessed | tf_op | source)
XLA Modules:
  0.0 119.1 jit_solution(13355934888414321919)
XLA Ops:
  0.6 2.5 %shard_map.68 = (f32[416,128]{1,0:T(8,128)}, f32[512,128]{1,0:T(8,128)S(1)}) custom-call(f32[1,200]{1,0:T(1,128)} %refs_0_.3, f32[1,10,2,200]{3,2,1,0:T(2,128)} %bitcast.11, s32[1,2]{1,0:T(1,128)} %refs_2_.3), custom_call_target="tpu_custom_call" | custom-call | tf_op jit(solution)/shard_map/pallas_call | solution.py:612
  3.1 0.0 copy-start
  3.1 33.2 %all-to-all-start = ((f32[32,1,1664]{2,1,0:T(1,128)}), f32[32,1,1664]{2,1,0:T(1,128)S(1)}, u32[]{:S(2)}, u32[]{:S(2)}) async-start(f32[32,1,1664]{2,1,0:T(1,128)} %bitcast.1), calls=%async_computation | async-start | bytes 425984 | tf_op jit(solution)/shard_map/all_to_all | solution.py:608
  36.3 0.0 copy-done
  36.4 0.0 copy-start.1
  36.4 0.2 copy.10.refs_3_
  36.6 0.5 copy-done.1
  37.1 0.2 copy.11.refs_4_
  37.4 1.4 %shard_map.69 = (f32[4,100,128]{2,1,0:T(8,128)S(1)}, f32[2,208,256]{2,1,0:T(8,128)S(1)}, bf16[208,96]{1,0:T(8,128)(2,1)S(1)}, f32[128,512]{1,0:T(8,128)S(1)}, bf...) custom-call(f32[1,200]{1,0:T(1,128)} %refs_0_.3, f32[1,10,2,200]{3,2,1,0:T(2,128)} %bitcast.12, s32[1,2]{1,0:T(1,128)} %refs_2_.3, ...), custom_call_target="tpu_custom_call" | custom-call | tf_op jit(solution)/shard_map/pallas_call | solution.py:613
  38.7 33.8 %all-to-all-done = f32[32,1,1664]{2,1,0:T(1,128)S(1)} async-done(((f32[32,1,1664]{2,1,0:T(1,128)}), f32[32,1,1664]{2,1,0:T(1,128)S(1)}, u32[]{:S(2)}, u32[]{:S(2)}) %all-to-all-start) | async-done | bytes 213024 | tf_op jit(solution)/shard_map/all_to_all | solution.py:608
  72.6 2.4 %collective-permute-start = (f32[416,128]{1,0:T(8,128)S(1)}, f32[416,128]{1,0:T(8,128)S(1)}, u32[]{:S(2)}, u32[]{:S(2)}) collective-permute-start(f32[416,128]{1,0:T(8,128)S(1)} %bitcast.7), channel_id=1, source_target_pairs={{0,1},{1,0},{2,3},{3,2},{4,5},{5,4},{6,7},{7,6},{8,9},{9,8},{10,11... | collective-permute-start | bytes 638984 | tf_op jit(solution)/shard_map/ppermute | solution.py:616
  75.0 0.7 shard_map.70.refs_2_
  75.7 0.4 collective-permute-done.refs_0_
  76.1 1.6 %shard_map.71.refs_7_ = f32[224,128]{1,0:T(8,128)S(1)} custom-call(f32[416,128]{1,0:T(8,128)S(1)} %collective-permute-done.refs_0_, f32[400,128]{1,0:T(8,128)S(1)} %get-tuple-element.35.refs_1_, f32[200,128]{1,0:T(8,128)S(1)} %shard_map.70.refs_2_), custom_call_target="tpu_custom_call" | custom-call | tf_op jit(solution)/shard_map/pallas_call | solution.py:617
  77.7 32.2 %all_to_all.10 = f32[32,1,896]{2,1,0:T(1,128)S(1)} all-to-all(f32[32,1,896]{2,1,0:T(1,128)S(1)} %bitcast.6), channel_id=1, replica_groups=mesh['parts'=4,'z'=32,'core'=2] {'z'}, dimensions={0} | all-to-all | bytes 229376 | tf_op jit(solution)/shard_map/all_to_all | solution.py:608
  109.8 2.0 %collective-permute-start.1 = (f32[224,128]{1,0:T(8,128)S(1)}, f32[224,128]{1,0:T(8,128)S(1)}, u32[]{:S(2)}, u32[]{:S(2)}) collective-permute-start(f32[224,128]{1,0:T(8,128)S(1)} %bitcast.9), channel_id=1, source_target_pairs={{0,1},{1,0},{2,3},{3,2},{4,5},{5,4},{6,7},{7,6},{8,9},{9,8},{10,11... | collective-permute-start | bytes 344072 | tf_op jit(solution)/shard_map/ppermute | solution.py:619
  111.8 1.0 shard_map.72
  112.8 0.0 collective-permute-done.1.refs_8_
  112.8 6.3 %shard_map.73 = (f32[1,2,200,200]{3,2,1,0:T(8,128)}, f32[2,10,4,10]{3,2,1,0:T(4,128)}) custom-call(f32[4,100,128]{2,1,0:T(8,128)S(1)} %get-tuple-element.29.refs_1_.refs_0_, f32[2,208,256]{2,1,0:T(8,128)S(1)} %get-tuple-element.30.refs_1_, bf16[208,96]{1,0:T(8,128)(2,1)S(1)} %get-tuple-element.31.refs_2_, f32[128,512]{1,0:T(8,128)S(1)} %get-tuple-element.32.refs_3_, ...), custom_call_target="tpu_custom_call" | custom-call | tf_op jit(solution)/shard_map/pallas_call | solution.py:620
Async XLA Ops:
  3.1 33.2 %copy-start = (f32[2,10,10,4]{2,3,1,0:T(4,128)S(1)}, f32[2,10,10,4]{2,3,1,0:T(4,128)}, u32[]{:S(2)}) copy-start(f32[2,10,10,4]{2,3,1,0:T(4,128)} %param.8) | copy-start | bytes 9604
  3.1 69.4 %all-to-all-start = ((f32[32,1,1664]{2,1,0:T(1,128)}), f32[32,1,1664]{2,1,0:T(1,128)S(1)}, u32[]{:S(2)}, u32[]{:S(2)}) async-start(f32[32,1,1664]{2,1,0:T(1,128)} %bitcast.1), calls=%async_computation | async-start | bytes 425984 | tf_op jit(solution)/shard_map/all_to_all | solution.py:608
  36.4 0.8 copy-start.1
  72.6 3.5 %collective-permute-start = (f32[416,128]{1,0:T(8,128)S(1)}, f32[416,128]{1,0:T(8,128)S(1)}, u32[]{:S(2)}, u32[]{:S(2)}) collective-permute-start(f32[416,128]{1,0:T(8,128)S(1)} %bitcast.7), channel_id=1, source_target_pairs={{0,1},{1,0},{2,3},{3,2},{4,5},{5,4},{6,7},{7,6},{8,9},{9,8},{10,11... | collective-permute-start | bytes 638984 | tf_op jit(solution)/shard_map/ppermute | solution.py:616
  109.8 3.0 %collective-permute-start.1 = (f32[224,128]{1,0:T(8,128)S(1)}, f32[224,128]{1,0:T(8,128)S(1)}, u32[]{:S(2)}, u32[]{:S(2)}) collective-permute-start(f32[224,128]{1,0:T(8,128)S(1)} %bitcast.9), channel_id=1, source_target_pairs={{0,1},{1,0},{2,3},{3,2},{4,5},{5,4},{6,7},{7,6},{8,9},{9,8},{10,11... | collective-permute-start | bytes 344072 | tf_op jit(solution)/shard_map/ppermute | solution.py:619
